TPU v7x, 32 devices: a whole 2x2x4 slice. The times are simulated.
32 devices in a mesh: grp: 2 (over x), pp: 4 (over z), dp: 4 (over y, core).
Axes of the slice: x: 2, y: 2, z: 4, core: 2. Of those that a mesh axis runs over, the one named last changes fastest.
Arguments:
- dy: bfloat16 [8, 256, 1024], P(('grp', 'pp'), 'dp'), parts along dimension 0
- xs: bfloat16 [8, 4, 1, 256, 1024], P(('grp', 'pp'), None, None, 'dp'), parts along dimension 0
- hs: bfloat16 [8, 4, 1, 256, 4096], P(('grp', 'pp'), None, None, 'dp'), parts along dimension 0
- w1: bfloat16 [8, 1, 1024, 4096], P(('grp', 'pp')), parts along dimension 0
- w2: bfloat16 [8, 1, 4096, 1024], P(('grp', 'pp')), parts along dimension 0
- acc1: float32 [8, 4, 1, 1024, 4096], P(('grp', 'pp'), 'dp'), parts along dimension 0
- acc2: float32 [8, 4, 1, 4096, 1024], P(('grp', 'pp'), 'dp'), parts along dimension 0
Outputs:
- output 1: float32 [8, 1, 1024, 4096], P(('grp', 'pp'), None, 'dp'), parts along dimension 0
- output 2: float32 [8, 1, 4096, 1024], P(('grp', 'pp'), None, 'dp'), parts along dimension 0
- output 3: bfloat16 [8, 256, 1024], P(('grp', 'pp'), 'dp'), parts along dimension 0
There are 2 independent parts. A program takes and returns all parts, laid end to end along the dimension named above; each array names one.
All inputs are finite; a program needn't handle non-finite values.
Results may differ from a plain program's by a relative error of at most 0.005103.
Values are sent between devices in bfloat16 or wider.
A program may use at most 1 GiB of HBM per device.

v0:
```python
import jax
import jax.numpy as jnp
from jax import lax
from jax.sharding import PartitionSpec as P


def gelu_fn(v):
    return jax.nn.gelu(v, approximate=True)


def layer_back(g, x, h, wa, wb):
    act, act_vjp = jax.vjp(gelu_fn, h.astype(jnp.float32))
    u = jnp.einsum('td,fd->tf', g, wb, preferred_element_type=jnp.float32)
    dh = act_vjp(u)[0].astype(jnp.bfloat16)
    gx = (g.astype(jnp.float32) + jnp.einsum('tf,df->td', dh, wa, preferred_element_type=jnp.float32)).astype(jnp.bfloat16)
    dwa = jnp.einsum('td,tf->df', x, dh, preferred_element_type=jnp.float32)
    dwb = jnp.einsum('tf,td->fd', act.astype(jnp.bfloat16), g, preferred_element_type=jnp.float32)
    return gx, dwa, dwb


def stage_back(g, xj, hj, wa, wb, ga, gb):
    for k in reversed(range(wa.shape[0])):
        g, dwa, dwb = layer_back(g, xj[k], hj[k], wa[k], wb[k])
        ga = ga.at[k].add(dwa)
        gb = gb.at[k].add(dwb)
    return g, ga, gb


def reduce_avg(acc, ndp):
    nk, rows, cols = acc.shape
    pieces = acc.astype(jnp.bfloat16).reshape(nk, ndp, rows // ndp, cols)
    recv = lax.all_to_all(pieces, 'dp', 1, 1, tiled=True)
    return jnp.sum(recv, axis=1, dtype=jnp.float32) / ndp


def solution(mesh):
    npp = mesh.shape['pp']
    ndp = mesh.shape['dp']

    def body(dy, xs, hs, w1, w2, acc1, acc2):
        s = lax.axis_index('pp')
        g = dy[0]
        ga = acc1[0, 0]
        gb = acc2[0, 0]
        wa = w1[0]
        wb = w2[0]
        r1 = jnp.zeros((ga.shape[0], ga.shape[1] // ndp, ga.shape[2]), jnp.float32)
        r2 = jnp.zeros((gb.shape[0], gb.shape[1] // ndp, gb.shape[2]), jnp.float32)
        outs0 = []
        for t in range(npp):
            j = npp - 1 - s - t
            jc = jnp.maximum(j, 0)
            xj = lax.dynamic_index_in_dim(xs[0], jc, 0, keepdims=False)
            hj = lax.dynamic_index_in_dim(hs[0], jc, 0, keepdims=False)
            g, ga, gb = lax.cond(j >= 0, lambda c: stage_back(c[0], xj, hj, wa, wb, c[1], c[2]), lambda c: c, (g, ga, gb))
            r1, r2 = lax.cond(j == 0, lambda c: (reduce_avg(c[0], ndp), reduce_avg(c[1], ndp)), lambda c: (c[2], c[3]), (ga, gb, r1, r2))
            outs0.append(g)
            if t < npp - 1:
                g = lax.ppermute(g, 'pp', [(r, r - 1) for r in range(1, npp - t)])
        dx_local = jnp.where(s == 0, outs0[npp - 1], jnp.zeros_like(g))
        for jj in range(1, npp):
            dx_local = dx_local + lax.ppermute(outs0[npp - 1 - jj], 'pp', [(0, jj)])
        return r1[None], r2[None], dx_local[None]

    spec_row = P(('grp', 'pp'), 'dp', None)
    spec_saved = P(('grp', 'pp'), None, None, 'dp', None)
    spec_w = P(('grp', 'pp'), None, None, None)
    spec_acc = P(('grp', 'pp'), 'dp', None, None, None)
    spec_g = P(('grp', 'pp'), None, 'dp', None)
    return jax.shard_map(body, mesh=mesh, in_specs=(spec_row, spec_saved, spec_saved, spec_w, spec_w, spec_acc, spec_acc), out_specs=(spec_g, spec_g, spec_row), check_vma=False)
```

profile of v0, /device:TPU:1, one launch (start us, length us, event | category | flops | bytes accessed | tf_op | source)
XLA Modules:
  0.0 419.7 jit_solution(5409280253008821770)
XLA Ops:
  0.6 12.6 %copy.54 = f32[1,1,1,1024,4096]{4,3,2,1,0:T(8,128)} copy(f32[1,1,1,1024,4096]{4,3,2,1,0:T(8,128)} %param.44) | data formatting | bytes 33554432
  17.1 6.5 %copy.55 = f32[1,1,1,4096,1024]{4,3,2,1,0:T(8,128)} copy(f32[1,1,1,4096,1024]{4,3,2,1,0:T(8,128)S(1)} %copy-done.6) | data formatting | bytes 33554432
  23.6 34.2 %conditional.8 = (bf16[64,1024]{1,0:T(8,128)(2,1)}, f32[1,1024,4096]{2,1,0:T(8,128)}, f32[1,4096,1024]{2,1,0:T(8,128)}) conditional(s32[]{:T(128)} %convert_element_type.188, (bf16[64,1024]{1,0:T(8,128)(2,1)S(1)}, f32[1,1024,4096]{2,1,0:T(8,128)}, f32[1,4096,1024]{2,1,0:T(8,128)}) %tuple.160, (bf16[64,1024]{1,0:T(8,128)(2,1)S(1)}, ...), branch_computations={%region_0.1_spmd, %region_1.2_spmd} | conditional | flops 2164195328 | bytes 238158016 | solution.py:55
  23.6 6.4 %fusion.13 = bf16[64,4096]{1,0:T(8,128)(2,1)S(1)} fusion(bf16[64,1024]{1,0:T(8,128)(2,1)S(1)} %get-tuple-element.388, bf16[1,1,4096,1024]{3,2,1,0:T(8,128)(2,1)} %get-tuple-element.389, bf16[1,4,1,64,4096]{4,3,2,1,0:T(8,128)(2,1)S(1)} %get-tuple-element.390, s32[]{:T(128)S(6)} %max.16), kind=kOutput, calls=%fused_computation.16 | convolution fusion | flops 542375936 | bytes 9568260 | tf_op jit(solution)/shard_map/cond/branch_1_fun/td,fd->tf/dot_general | solution.py:13
  33.3 14.0 %bitcast_add_fusion.1 = f32[1,1024,4096]{2,1,0:T(8,128)} fusion(f32[1,1024,4096]{2,1,0:T(8,128)} %get-tuple-element.393, bf16[64,4096]{1,0:T(8,128)(2,1)S(1)} %fusion.13, bf16[1,4,1,64,1024]{4,3,2,1,0:T(8,128)(2,1)S(1)} %get-tuple-element.394, s32[]{:T(128)S(6)} %max.16), kind=kOutput, calls=%fused_computation.1 | convolution fusion | flops 541065216 | bytes 34209796 | tf_op jit(solution)/shard_map/cond/branch_1_fun/td,tf->df/dot_general | solution.py:16
  65.0 32.1 %conditional.10 = (bf16[64,1024]{1,0:T(8,128)(2,1)}, f32[1,1024,4096]{2,1,0:T(8,128)}, f32[1,4096,1024]{2,1,0:T(8,128)}) conditional(s32[]{:T(128)} %convert_element_type.189, (bf16[64,1024]{1,0:T(8,128)(2,1)S(1)}, f32[1,1024,4096]{2,1,0:T(8,128)}, f32[1,4096,1024]{2,1,0:T(8,128)}) %tuple.119, (bf16[64,1024]{1,0:T(8,128)(2,1)S(1)}, ...), branch_computations={%region_6.7_spmd, %region_7.8_spmd} | conditional | flops 2164195328 | bytes 171049120 | solution.py:55
  65.2 6.4 %fusion.50 = bf16[64,4096]{1,0:T(8,128)(2,1)S(1)} fusion(bf16[64,1024]{1,0:T(8,128)(2,1)S(1)} %get-tuple-element.398, bf16[1,1,4096,1024]{3,2,1,0:T(8,128)(2,1)} %get-tuple-element.399, bf16[1,4,1,64,4096]{4,3,2,1,0:T(8,128)(2,1)S(1)} %get-tuple-element.400, s32[]{:T(128)S(6)} %max.17), kind=kOutput, calls=%fused_computation.57 | convolution fusion | flops 542375936 | bytes 9568260 | tf_op jit(solution)/shard_map/cond/branch_1_fun/td,fd->tf/dot_general | solution.py:13
  74.9 14.0 %bitcast_add_fusion.3 = f32[1,1024,4096]{2,1,0:T(8,128)} fusion(f32[1,1024,4096]{2,1,0:T(8,128)} %get-tuple-element.403, bf16[64,4096]{1,0:T(8,128)(2,1)S(1)} %fusion.50, bf16[1,4,1,64,1024]{4,3,2,1,0:T(8,128)(2,1)S(1)} %get-tuple-element.404, s32[]{:T(128)S(6)} %max.17), kind=kOutput, calls=%fused_computation.42 | convolution fusion | flops 541065216 | bytes 34209796 | tf_op jit(solution)/shard_map/cond/branch_1_fun/td,tf->df/dot_general | solution.py:16
  89.0 8.1 %bitcast_add_fusion.2 = f32[1,4096,1024]{2,1,0:T(8,128)} fusion(f32[1,4096,1024]{2,1,0:T(8,128)S(1)} %bitcast.156, bf16[64,1024]{1,0:T(8,128)(2,1)S(1)} %get-tuple-element.398, bf16[1,4,1,64,4096]{4,3,2,1,0:T(8,128)(2,1)S(1)} %get-tuple-element.400, s32[]{:T(128)S(6)} %max.17), kind=kOutput, calls=%fused_computation.41 | convolution fusion | flops 543686656 | bytes 34209796 | tf_op jit(solution)/shard_map/cond/branch_1_fun/tf,td->fd/dot_general | solution.py:17
  102.8 38.1 %conditional.12 = (bf16[64,1024]{1,0:T(8,128)(2,1)}, f32[1,1024,4096]{2,1,0:T(8,128)}, f32[1,4096,1024]{2,1,0:T(8,128)}) conditional(s32[]{:T(128)} %convert_element_type.190, (bf16[64,1024]{1,0:T(8,128)(2,1)S(1)}, f32[1,1024,4096]{2,1,0:T(8,128)}, f32[1,4096,1024]{2,1,0:T(8,128)}) %tuple.122, (bf16[64,1024]{1,0:T(8,128)(2,1)S(1)}, ...), branch_computations={%region_12.13_spmd, %region_13.14_spmd} | conditional | flops 2164195328 | bytes 120717384 | solution.py:55
  103.2 6.4 %fusion.87 = bf16[64,4096]{1,0:T(8,128)(2,1)S(1)} fusion(bf16[64,1024]{1,0:T(8,128)(2,1)S(1)} %get-tuple-element.408, bf16[1,1,4096,1024]{3,2,1,0:T(8,128)(2,1)} %get-tuple-element.409, bf16[1,4,1,64,4096]{4,3,2,1,0:T(8,128)(2,1)S(1)} %get-tuple-element.410, s32[]{:T(128)S(6)} %max.18), kind=kOutput, calls=%fused_computation.98 | convolution fusion | flops 542375936 | bytes 9568260 | tf_op jit(solution)/shard_map/cond/branch_1_fun/td,fd->tf/dot_general | solution.py:13
  112.9 14.0 %bitcast_add_fusion.5 = f32[1,1024,4096]{2,1,0:T(8,128)} fusion(f32[1,1024,4096]{2,1,0:T(8,128)} %get-tuple-element.413, bf16[64,4096]{1,0:T(8,128)(2,1)S(1)} %fusion.87, bf16[1,4,1,64,1024]{4,3,2,1,0:T(8,128)(2,1)S(1)} %get-tuple-element.414, s32[]{:T(128)S(6)} %max.18), kind=kOutput, calls=%fused_computation.83 | convolution fusion | flops 541065216 | bytes 34209796 | tf_op jit(solution)/shard_map/cond/branch_1_fun/td,tf->df/dot_general | solution.py:16
  126.9 14.0 %bitcast_add_fusion.4 = f32[1,4096,1024]{2,1,0:T(8,128)} fusion(f32[1,4096,1024]{2,1,0:T(8,128)} %get-tuple-element.415, bf16[64,1024]{1,0:T(8,128)(2,1)S(1)} %get-tuple-element.408, bf16[1,4,1,64,4096]{4,3,2,1,0:T(8,128)(2,1)S(1)} %get-tuple-element.410, s32[]{:T(128)S(6)} %max.18), kind=kOutput, calls=%fused_computation.82 | convolution fusion | flops 543686656 | bytes 34209796 | tf_op jit(solution)/shard_map/cond/branch_1_fun/tf,td->fd/dot_general | solution.py:17
  154.7 11.4 %conditional.13 = ((f32[1,256,4096]{2,1,0:T(8,128)}, f32[1,1024,1024]{2,1,0:T(8,128)})) conditional(s32[]{:T(128)} %convert_element_type.185, (f32[1,256,4096]{2,1,0:T(8,128)}, f32[1,1024,1024]{2,1,0:T(8,128)}) %get-tuple-element.511, (f32[1,1024,4096]{2,1,0:T(8,128)}, f32[1,4096,1024]{2,1,0:T(8,128)}) %tuple.124), branch_computations={%region_14.15_spmd, %region_15.18_spmd} | conditional | flops 25165824 | bytes 142606432 | solution.py:56
  166.0 34.2 %conditional.14 = ((bf16[64,1024]{1,0:T(8,128)(2,1)S(1)}, f32[1,1024,4096]{2,1,0:T(8,128)}, f32[1,4096,1024]{2,1,0:T(8,128)})) conditional(s32[]{:T(128)} %convert_element_type.191, (bf16[64,1024]{1,0:T(8,128)(2,1)S(1)}, f32[1,1024,4096]{2,1,0:T(8,128)}, f32[1,4096,1024]{2,1,0:T(8,128)}) %tuple.125, (bf16[64,1024]{1,0:T(8,128)(2,1)S(1)}, ...), branch_computations={%region_18.19_spmd, %region_19.20_spmd} | conditional | flops 2164195328 | bytes 154271840 | solution.py:55
  166.1 14.1 %bitcast_add_fusion.6 = f32[1,4096,1024]{2,1,0:T(8,128)} fusion(f32[1,4096,1024]{2,1,0:T(8,128)} %get-tuple-element.425, bf16[64,1024]{1,0:T(8,128)(2,1)S(1)} %get-tuple-element.418, bf16[1,4,1,64,4096]{4,3,2,1,0:T(8,128)(2,1)S(1)} %get-tuple-element.420, s32[]{:T(128)S(6)} %max.19), kind=kOutput, calls=%fused_computation.123 | convolution fusion | flops 543686656 | bytes 34209796 | tf_op jit(solution)/shard_map/cond/branch_1_fun/tf,td->fd/dot_general | solution.py:17
  186.3 14.0 %bitcast_add_fusion.7 = f32[1,1024,4096]{2,1,0:T(8,128)} fusion(f32[1,1024,4096]{2,1,0:T(8,128)} %get-tuple-element.423, bf16[64,4096]{1,0:T(8,128)(2,1)S(1)} %fusion.124, bf16[1,4,1,64,1024]{4,3,2,1,0:T(8,128)(2,1)S(1)} %get-tuple-element.424, s32[]{:T(128)S(6)} %max.19), kind=kOutput, calls=%fused_computation.124 | convolution fusion | flops 541065216 | bytes 34209796 | tf_op jit(solution)/shard_map/cond/branch_1_fun/td,tf->df/dot_general | solution.py:16
  200.3 217.1 %conditional.15 = (f32[1,1,256,4096]{3,2,1,0:T(8,128)}, f32[1,1,1024,1024]{3,2,1,0:T(8,128)}) conditional(s32[]{:T(128)} %convert_element_type.184, (f32[1,256,4096]{2,1,0:T(8,128)}, f32[1,1024,1024]{2,1,0:T(8,128)}) %get-tuple-element.512, (f32[1,1024,4096]{2,1,0:T(8,128)}, f32[1,4096,1024]{2,1,0:T(8,128)}) %tuple.127), branch_computations={%region_20.21_spmd, %region_21.24_spmd} | conditional | flops 25165824 | bytes 142606416 | solution.py:56
  200.3 9.1 %convert_element_type.172 = bf16[1,1024,4096]{2,1,0:T(8,128)(2,1)} convert(f32[1,1024,4096]{2,1,0:T(8,128)} %get-tuple-element.428) | non-fusion elementwise | flops 4194304 | bytes 25165824 | tf_op jit(solution)/shard_map/cond/branch_1_fun/convert_element_type | solution.py:31
  209.3 8.6 %all-to-all-start.6 = ((bf16[1,4,256,4096]{3,2,0,1:T(8,128)(2,1)}), bf16[1,4,256,4096]{3,2,0,1:T(8,128)(2,1)}, u32[]{:S(2)}, u32[]{:S(2)}) async-start(bf16[1,4,256,4096]{3,2,0,1:T(8,128)(2,1)} %bitcast.166), calls=%async_computation.6 | async-start | bytes 16777216 | tf_op jit(solution)/shard_map/cond/branch_1_fun/all_to_all | solution.py:32
  217.9 9.0 %convert_element_type.174 = bf16[1,4096,1024]{2,1,0:T(8,128)(2,1)} convert(f32[1,4096,1024]{2,1,0:T(8,128)} %get-tuple-element.429) | non-fusion elementwise | flops 4194304 | bytes 25165824 | tf_op jit(solution)/shard_map/cond/branch_1_fun/convert_element_type | solution.py:31
  227.0 83.0 %all-to-all-done.6 = bf16[1,4,256,4096]{3,2,0,1:T(8,128)(2,1)} async-done(((bf16[1,4,256,4096]{3,2,0,1:T(8,128)(2,1)}), bf16[1,4,256,4096]{3,2,0,1:T(8,128)(2,1)}, u32[]{:S(2)}, u32[]{:S(2)}) %all-to-all-start.6) | async-done | bytes 8388640 | tf_op jit(solution)/shard_map/cond/branch_1_fun/all_to_all | solution.py:32
  309.9 6.8 %all-to-all-start.7 = ((bf16[1,4,1024,1024]{3,2,0,1:T(8,128)(2,1)}), bf16[1,4,1024,1024]{3,2,0,1:T(8,128)(2,1)}, u32[]{:S(2)}, u32[]{:S(2)}) async-start(bf16[1,4,1024,1024]{3,2,0,1:T(8,128)(2,1)} %bitcast.161), calls=%async_computation.7 | async-start | bytes 16777216 | tf_op jit(solution)/shard_map/cond/branch_1_fun/all_to_all | solution.py:32
  324.4 84.3 %all-to-all-done.7 = bf16[1,4,1024,1024]{3,2,0,1:T(8,128)(2,1)} async-done(((bf16[1,4,1024,1024]{3,2,0,1:T(8,128)(2,1)}), bf16[1,4,1024,1024]{3,2,0,1:T(8,128)(2,1)}, u32[]{:S(2)}, u32[]{:S(2)}) %all-to-all-start.7) | async-done | bytes 8388640 | tf_op jit(solution)/shard_map/cond/branch_1_fun/all_to_all | solution.py:32
  (65 shorter events, 79.7 us)
Async XLA Ops:
  0.6 16.4 %copy-start.6 = (f32[1,1,1,4096,1024]{4,3,2,1,0:T(8,128)S(1)}, f32[1,1,1,4096,1024]{4,3,2,1,0:T(8,128)}, u32[]{:S(2)}) copy-start(f32[1,1,1,4096,1024]{4,3,2,1,0:T(8,128)} %param.45) | copy-start | bytes 50331652
  17.1 6.5 %copy-start.7 = (bf16[1,4,1,64,4096]{4,3,2,1,0:T(8,128)(2,1)S(1)}, bf16[1,4,1,64,4096]{4,3,2,1,0:T(8,128)(2,1)}, u32[]{:S(2)}) copy-start(bf16[1,4,1,64,4096]{4,3,2,1,0:T(8,128)(2,1)} %param.41) | copy-start | bytes 6291460
  17.1 6.5 %copy-start.8 = (bf16[1,64,1024]{2,1,0:T(8,128)(2,1)S(1)}, bf16[1,64,1024]{2,1,0:T(8,128)(2,1)}, u32[]{:S(2)}) copy-start(bf16[1,64,1024]{2,1,0:T(8,128)(2,1)} %param.39) | copy-start | bytes 393220
  17.1 6.5 %copy-start.9 = (bf16[1,4,1,64,1024]{4,3,2,1,0:T(8,128)(2,1)S(1)}, bf16[1,4,1,64,1024]{4,3,2,1,0:T(8,128)(2,1)}, u32[]{:S(2)}) copy-start(bf16[1,4,1,64,1024]{4,3,2,1,0:T(8,128)(2,1)} %param.40) | copy-start | bytes 1572868
  23.6 6.4 %copy-start.2 = (bf16[1,1,1024,4096]{3,2,1,0:T(8,128)(2,1)S(1)}, bf16[1,1,1024,4096]{3,2,1,0:T(8,128)(2,1)}, u32[]{:S(2)}) copy-start(bf16[1,1,1024,4096]{3,2,1,0:T(8,128)(2,1)} %get-tuple-element.392) | copy-start | bytes 25165828 | tf_op jit(solution)/shard_map/cond
  30.0 17.4 %slice-start = ((s8[16777216]{0:T(1024)(128)(4,1)}), s8[4194304]{0:T(1024)(128)(4,1)S(1)}, s32[]{:S(2)}) async-start(s8[16777216]{0:T(1024)(128)(4,1)} %bitcast.153), calls=%async_computation.8 | async-start | bytes 8388608 | tf_op jit(solution)/shard_map/cond
  33.3 14.0 %slice-start.1 = ((s8[16777216]{0:T(1024)(128)(4,1)}), s8[4194304]{0:T(1024)(128)(4,1)S(1)}, s32[]{:S(2)}) async-start(s8[16777216]{0:T(1024)(128)(4,1)} %bitcast.153), calls=%async_computation.9 | async-start | bytes 8388608 | tf_op jit(solution)/shard_map/cond
  33.3 14.0 %slice-start.2 = ((s8[16777216]{0:T(1024)(128)(4,1)}), s8[4194304]{0:T(1024)(128)(4,1)S(1)}, s32[]{:S(2)}) async-start(s8[16777216]{0:T(1024)(128)(4,1)} %bitcast.153), calls=%async_computation.10 | async-start | bytes 8388608 | tf_op jit(solution)/shard_map/cond
  33.3 14.0 %slice-start.3 = ((s8[16777216]{0:T(1024)(128)(4,1)}), s8[4194304]{0:T(1024)(128)(4,1)S(1)}, s32[]{:S(2)}) async-start(s8[16777216]{0:T(1024)(128)(4,1)} %bitcast.153), calls=%async_computation.11 | async-start | bytes 8388608 | tf_op jit(solution)/shard_map/cond
  57.8 7.2 %collective-permute-start = (bf16[64,1024]{1,0:T(8,128)(2,1)}, bf16[64,1024]{1,0:T(8,128)(2,1)S(1)}, u32[]{:S(2)}, u32[]{:S(2)}) collective-permute-start(bf16[64,1024]{1,0:T(8,128)(2,1)} %get-tuple-element.449), channel_id=1, source_target_pairs={{4,0},{8,4},{12,8},{5,1},{9,5},{13,9},{6,2},{10,6},{14,10},{7,3},{... | collective-permute-start | bytes 393224 | tf_op jit(solution)/shard_map/ppermute | solution.py:59
  65.2 6.4 %copy-start.3 = (bf16[1,1,1024,4096]{3,2,1,0:T(8,128)(2,1)S(1)}, bf16[1,1,1024,4096]{3,2,1,0:T(8,128)(2,1)}, u32[]{:S(2)}) copy-start(bf16[1,1,1024,4096]{3,2,1,0:T(8,128)(2,1)} %get-tuple-element.402) | copy-start | bytes 25165828 | tf_op jit(solution)/shard_map/cond
  71.6 17.4 %slice-start.4 = ((s8[16777216]{0:T(1024)(128)(4,1)}), s8[4194304]{0:T(1024)(128)(4,1)S(1)}, s32[]{:S(2)}) async-start(s8[16777216]{0:T(1024)(128)(4,1)} %bitcast.155), calls=%async_computation.12 | async-start | bytes 8388608 | tf_op jit(solution)/shard_map/cond
  74.9 14.0 %slice-start.5 = ((s8[16777216]{0:T(1024)(128)(4,1)}), s8[4194304]{0:T(1024)(128)(4,1)S(1)}, s32[]{:S(2)}) async-start(s8[16777216]{0:T(1024)(128)(4,1)} %bitcast.155), calls=%async_computation.13 | async-start | bytes 8388608 | tf_op jit(solution)/shard_map/cond
  74.9 14.0 %slice-start.6 = ((s8[16777216]{0:T(1024)(128)(4,1)}), s8[4194304]{0:T(1024)(128)(4,1)S(1)}, s32[]{:S(2)}) async-start(s8[16777216]{0:T(1024)(128)(4,1)} %bitcast.155), calls=%async_computation.14 | async-start | bytes 8388608 | tf_op jit(solution)/shard_map/cond
  74.9 14.1 %slice-start.7 = ((s8[16777216]{0:T(1024)(128)(4,1)}), s8[4194304]{0:T(1024)(128)(4,1)S(1)}, s32[]{:S(2)}) async-start(s8[16777216]{0:T(1024)(128)(4,1)} %bitcast.155), calls=%async_computation.15 | async-start | bytes 8388608 | tf_op jit(solution)/shard_map/cond
  97.1 5.7 %collective-permute-start.1 = (bf16[64,1024]{1,0:T(8,128)(2,1)}, bf16[64,1024]{1,0:T(8,128)(2,1)S(1)}, u32[]{:S(2)}, u32[]{:S(2)}) collective-permute-start(bf16[64,1024]{1,0:T(8,128)(2,1)} %get-tuple-element.452), channel_id=1, source_target_pairs={{4,0},{8,4},{5,1},{9,5},{6,2},{10,6},{7,3},{11,7},{20,16},{24,20},... | collective-permute-start | bytes 393224 | tf_op jit(solution)/shard_map/ppermute | solution.py:59
  103.2 6.4 %copy-start.4 = (bf16[1,1,1024,4096]{3,2,1,0:T(8,128)(2,1)S(1)}, bf16[1,1,1024,4096]{3,2,1,0:T(8,128)(2,1)}, u32[]{:S(2)}) copy-start(bf16[1,1,1024,4096]{3,2,1,0:T(8,128)(2,1)} %get-tuple-element.412) | copy-start | bytes 25165828 | tf_op jit(solution)/shard_map/cond
  140.9 25.2 %collective-permute-start.2 = (bf16[64,1024]{1,0:T(8,128)(2,1)}, bf16[64,1024]{1,0:T(8,128)(2,1)S(1)}, u32[]{:S(2)}, u32[]{:S(2)}) collective-permute-start(bf16[64,1024]{1,0:T(8,128)(2,1)} %get-tuple-element.455), channel_id=1, source_target_pairs={{4,0},{5,1},{6,2},{7,3},{20,16},{21,17},{22,18},{23,19}} | collective-permute-start | bytes 393224 | tf_op jit(solution)/shard_map/ppermute | solution.py:59
  142.2 275.2 %collective-permute-start.5 = (bf16[64,1024]{1,0:T(8,128)(2,1)}, bf16[64,1024]{1,0:T(8,128)(2,1)}, u32[]{:S(2)}, u32[]{:S(2)}) collective-permute-start(bf16[64,1024]{1,0:T(8,128)(2,1)} %get-tuple-element.449), channel_id=1, source_target_pairs={{0,12},{1,13},{2,14},{3,15},{16,28},{17,29},{18,30},{19,31}} | collective-permute-start | bytes 393224 | tf_op jit(solution)/shard_map/ppermute | solution.py:62
  144.1 273.3 %collective-permute-start.4 = (bf16[64,1024]{1,0:T(8,128)(2,1)}, bf16[64,1024]{1,0:T(8,128)(2,1)}, u32[]{:S(2)}, u32[]{:S(2)}) collective-permute-start(bf16[64,1024]{1,0:T(8,128)(2,1)} %get-tuple-element.452), channel_id=1, source_target_pairs={{0,8},{1,9},{2,10},{3,11},{16,24},{17,25},{18,26},{19,27}} | collective-permute-start | bytes 393224 | tf_op jit(solution)/shard_map/ppermute | solution.py:62
  146.1 271.3 %collective-permute-start.3 = (bf16[64,1024]{1,0:T(8,128)(2,1)}, bf16[64,1024]{1,0:T(8,128)(2,1)}, u32[]{:S(2)}, u32[]{:S(2)}) collective-permute-start(bf16[64,1024]{1,0:T(8,128)(2,1)} %get-tuple-element.455), channel_id=1, source_target_pairs={{0,4},{1,5},{2,6},{3,7},{16,20},{17,21},{18,22},{19,23}} | collective-permute-start | bytes 393224 | tf_op jit(solution)/shard_map/ppermute | solution.py:62
  166.1 14.2 %copy-start.10 = (bf16[1,1,4096,1024]{3,2,1,0:T(8,128)(2,1)S(1)}, bf16[1,1,4096,1024]{3,2,1,0:T(8,128)(2,1)}, u32[]{:S(2)}) copy-start(bf16[1,1,4096,1024]{3,2,1,0:T(8,128)(2,1)} %get-tuple-element.419) | copy-start | bytes 25165828 | tf_op jit(solution)/shard_map/cond
  209.3 100.6 %all-to-all-start.6 = ((bf16[1,4,256,4096]{3,2,0,1:T(8,128)(2,1)}), bf16[1,4,256,4096]{3,2,0,1:T(8,128)(2,1)}, u32[]{:S(2)}, u32[]{:S(2)}) async-start(bf16[1,4,256,4096]{3,2,0,1:T(8,128)(2,1)} %bitcast.166), calls=%async_computation.6 | async-start | bytes 16777216 | tf_op jit(solution)/shard_map/cond/branch_1_fun/all_to_all | solution.py:32
  309.9 98.7 %all-to-all-start.7 = ((bf16[1,4,1024,1024]{3,2,0,1:T(8,128)(2,1)}), bf16[1,4,1024,1024]{3,2,0,1:T(8,128)(2,1)}, u32[]{:S(2)}, u32[]{:S(2)}) async-start(bf16[1,4,1024,1024]{3,2,0,1:T(8,128)(2,1)} %bitcast.161), calls=%async_computation.7 | async-start | bytes 16777216 | tf_op jit(solution)/shard_map/cond/branch_1_fun/all_to_all | solution.py:32
  (2 other events, 9.1 us)
where the time goes:
time: 428 us; the launch traced here: 420 us
  waiting for transfers between devices  178 us (42%)
  matrix products  131 us (31%)
  other arithmetic  35.9 us (8%)
  local copies, waits for them, and re-layouts  34.3 us (8%)
  starting transfers between devices  26.5 us (6%)
  loops' own time  12.7 us (3%)
    all_to_all x2, waiting for transfers between devices, reduce_avg(): recv = lax.all_to_all(pieces, 'dp', 1, 1, tiled=True)  167 us
    dot_general x4, matrix products, layer_back(): dwa = jnp.einsum('td,tf->df', x, dh, preferred_element_type=jnp.float32)  56 us
    dot_general x4, matrix products, layer_back(): jnp.einsum('tf,td->fd', act.astype(jnp.bfloat16), g, preferred_element_ty...  40.9 us
    unnamed x10, local copies, waits for them, and re-layouts  23 us
    dot_general x4, matrix products, layer_back(): u = jnp.einsum('td,fd->tf', g, wb, preferred_element_type=jnp.float32)  22 us
    convert_element_type x2, other arithmetic, reduce_avg(): pieces = acc.astype(jnp.bfloat16).reshape(nk, ndp, rows // ndp, cols)  18.1 us
    all_to_all x2, starting transfers between devices, reduce_avg(): recv = lax.all_to_all(pieces, 'dp', 1, 1, tiled=True)  15.4 us
    dot_general x4, matrix products, layer_back(): jnp.einsum('tf,df->td', dh, wa, preferred_element_type=jnp.float32)  12.7 us
  transfers between devices with their start and end apart: 8, of which 4 were waited for; matrix products, arithmetic and copies ran while one was open for 17% of the time, Pallas kernels for 0%

commit v1 on v0

v1 whole, which is shorter than its diff:
```python
import functools

import jax
import jax.numpy as jnp
from jax import lax
from jax.experimental import pallas as pl
from jax.experimental.pallas import tpu as pltpu
from jax.sharding import PartitionSpec as P

MESH = pl.DeviceIdType.MESH
NN = (((1,), (0,)), ((), ()))
NT = (((1,), (1,)), ((), ()))
SQRT_2_OVER_PI = 0.7978845608028654
BF16 = jnp.bfloat16
F32 = jnp.float32


def dot(a, b, dims):
    return lax.dot_general(a, b, dims, preferred_element_type=F32)


def kernel(npp, ndp, tok, nchunk, dy, xs, hs, w1, w2, acc1, acc2, g1, g2, dx,
           w1v, w2v, recv1, recv2, hv, xv, act, slope, dht, xt, gall, gin, gout, dxin, ident,
           stage1, stage2, out1, out2,
           ld_sem, h_sem, w2_sem, w1_sem, st1_sem, st2_sem, o1_sem, o2_sem,
           hop_send, hop_recv, dx_recv, dx_sem, send1, recv1_sem, send2, recv2_sem):
    s = lax.axis_index('pp')
    p = lax.axis_index('dp')
    dm, ff = w1v.shape
    ntok = npp * tok
    blk = ident.shape[0]
    nw2 = 8
    w2rows = ff // nw2
    nblk = dm // blk
    q1 = dm // ndp
    q2 = ff // ndp
    c1 = ff // nchunk
    c2 = q2 // nchunk

    far = (p + 2) % ndp
    peer = (p, p + 1 - 2 * (p % 2), far, far + 1 - 2 * (far % 2))

    def w2_copy(i):
        rows = pl.ds(i * w2rows, w2rows)
        return pltpu.make_async_copy(w2.at[rows, :], w2v.at[rows, :], w2_sem.at[i])

    def w1_copy(i):
        rows = pl.ds(i * blk, blk)
        return pltpu.make_async_copy(w1.at[rows, :], w1v.at[rows, :], w1_sem.at[i])

    def acc1_copy(i, k):
        slot = i % 2
        src = acc1.at[pl.ds(peer[k] * q1, q1), pl.ds(pl.multiple_of(i * c1, c1), c1)]
        return pltpu.make_async_copy(src, stage1.at[slot, k], st1_sem.at[slot, k])

    def acc2_copy(i, k):
        slot = i % 2
        src = acc2.at[pl.ds(peer[k] * q2 + i * c2, c2), :]
        return pltpu.make_async_copy(src, stage2.at[slot, k], st2_sem.at[slot, k])

    def h_copy(j):
        rows = pl.ds(j * tok, tok)
        return pltpu.make_async_copy(hs.at[rows, :], hv.at[rows, :], h_sem.at[j])

    x_copy = pltpu.make_async_copy(xs, xv, ld_sem.at[0])
    for j in range(npp):
        @pl.when(j < npp - s)
        def _():
            h_copy(j).start()
    for c in range(nblk):
        pltpu.make_async_copy(dy.at[:, pl.ds(c * blk, blk)], gin.at[0, c], hop_recv.at[0, c]).start()
    for i in range(nw2):
        w2_copy(i).start()
    for i in range(nblk):
        w1_copy(i).start()
    x_copy.start()
    for i in range(2):
        for k in range(ndp):
            acc2_copy(i, k).start()
    for i in range(2):
        for k in range(ndp):
            acc1_copy(i, k).start()

    barrier = pltpu.get_barrier_semaphore()
    for k in range(1, ndp):
        pl.semaphore_signal(barrier, inc=1, device_id={'dp': peer[k]}, device_id_type=MESH)
    for k in range(1, npp):
        pl.semaphore_signal(barrier, inc=1, device_id={'pp': (s + k) % npp}, device_id_type=MESH)

    rid = lax.broadcasted_iota(jnp.int32, (blk, blk), 0)
    cid = lax.broadcasted_iota(jnp.int32, (blk, blk), 1)
    ident[...] = jnp.where(rid == cid, 1.0, 0.0).astype(BF16)
    gall[...] = jnp.zeros_like(gall)

    for j in range(npp):
        @pl.when(j < npp - s)
        def _():
            h_copy(j).wait()

        @pl.when(j >= npp - s)
        def _():
            hv[j * tok:(j + 1) * tok, :] = jnp.zeros((tok, ff), BF16)

    def gelu_step(i, _):
        rows = pl.ds(pl.multiple_of(i * blk, blk), blk)
        h = dot(ident[...], hv[:, rows], NT)
        t = jnp.tanh(SQRT_2_OVER_PI * (h + 0.044715 * (h * h * h)))
        cdf = 0.5 * (1.0 + t)
        act[rows, :] = (h * cdf).astype(BF16)
        inner = SQRT_2_OVER_PI * (1.0 + (3.0 * 0.044715) * (h * h))
        slope[rows, :] = cdf + 0.5 * h * ((1.0 + t) * (1.0 - t)) * inner
        return 0

    lax.fori_loop(0, ff // blk, gelu_step, 0)

    pl.semaphore_wait(barrier, ndp - 1 + npp - 1)

    def hop_copy(t, c, to):
        return pltpu.make_async_remote_copy(
            src_ref=gout.at[t, c], dst_ref=gin.at[t + 1, c], send_sem=hop_send.at[t, c], recv_sem=hop_recv.at[t + 1, c],
            device_id={'pp': to}, device_id_type=MESH)

    def dx_copy(t, c, to):
        return pltpu.make_async_remote_copy(
            src_ref=gout.at[t, c], dst_ref=dxin.at[c], send_sem=hop_send.at[t, c], recv_sem=dx_recv.at[c],
            device_id={'pp': to}, device_id_type=MESH)

    for t in range(npp):
        j = npp - 1 - t - s

        @pl.when(j >= 0)
        def _(t=t, j=j):
            trows = pl.ds(pl.multiple_of(j * tok, tok), tok)
            for c in range(nblk):
                if t == 0:
                    pltpu.make_async_copy(dy.at[:, pl.ds(c * blk, blk)], gin.at[0, c], hop_recv.at[0, c]).wait()
                else:
                    hop_copy(t - 1, c, s).wait_recv()
                gall[trows, c * blk:(c + 1) * blk] = gin[t, c]

            def u_step(i, _):
                if t == 0:
                    w2_copy(i).wait()
                rows = pl.ds(pl.multiple_of(i * w2rows, w2rows), w2rows)
                u = dot(w2v[rows, :], gall[...], NT)
                dht[rows, :] = (slope[rows, :] * u).astype(BF16)
                return 0

            lax.fori_loop(0, nw2, u_step, 0)

            def gx_step(c, _):
                if t == 0:
                    w1_copy(c).wait()
                rows = pl.ds(pl.multiple_of(c * blk, blk), blk)
                z = dot(ident[...], gall[:, rows], NT) + dot(w1v[rows, :], dht[...], NN)
                zt = dot(ident[trows, :], z.astype(BF16), NT)
                gout[t, c] = zt.astype(BF16)

                if t < npp - 1:
                    @pl.when(s > 0)
                    def _():
                        hop_copy(t, c, jnp.maximum(s - 1, 0)).start()

                    @pl.when(s == 0)
                    def _():
                        dx_copy(t, c, npp - 1 - t).start()
                return 0

            lax.fori_loop(0, nblk, gx_step, 0)

    x_copy.wait()
    for c in range(nblk):
        rows = pl.ds(c * blk, blk)
        xt[rows, :] = dot(ident[...], xv[:, rows], NT).astype(BF16)

    def send2_copy(i, k):
        return pltpu.make_async_remote_copy(
            src_ref=w2v.at[pl.ds(peer[k] * q2 + i * c2, c2), :], dst_ref=recv2.at[k - 1, i],
            send_sem=send2.at[k - 1, i], recv_sem=recv2_sem.at[k - 1, i], device_id={'dp': peer[k]}, device_id_type=MESH)

    def send1_copy(i, k):
        return pltpu.make_async_remote_copy(
            src_ref=w1v.at[pl.ds(peer[k] * q1, q1), pl.ds(pl.multiple_of(i * c1, c1), c1)], dst_ref=recv1.at[k - 1, i],
            send_sem=send1.at[k - 1, i], recv_sem=recv1_sem.at[k - 1, i], device_id={'dp': peer[k]}, device_id_type=MESH)

    order = (2, 3, 1, 0)

    def a2_step(i, _):
        slot = i % 2
        for k in order:
            acc2_copy(i, k).wait()
            rows = pl.ds(pl.multiple_of(peer[k] * q2 + i * c2, c2), c2)
            w2v[rows, :] = (stage2[slot, k] + dot(act[rows, :], gall[...], NN)).astype(BF16)
        for k in order[:-1]:
            send2_copy(i, k).start()

        @pl.when(i + 2 < nchunk)
        def _():
            for k in range(ndp):
                acc2_copy(i + 2, k).start()
        return 0

    lax.fori_loop(0, nchunk, a2_step, 0)

    def a1_step(i, _):
        slot = i % 2
        cols = pl.ds(pl.multiple_of(i * c1, c1), c1)
        for k in order:
            acc1_copy(i, k).wait()
            rows = pl.ds(pl.multiple_of(peer[k] * q1, q1), q1)
            w1v[rows, cols] = (stage1[slot, k] + dot(xt[rows, :], dht[cols, :], NT)).astype(BF16)
        for k in order[:-1]:
            send1_copy(i, k).start()

        @pl.when(i + 2 < nchunk)
        def _():
            for k in range(ndp):
                acc1_copy(i + 2, k).start()
        return 0

    lax.fori_loop(0, nchunk, a1_step, 0)

    for c in range(nblk):
        out = dx.at[:, pl.ds(c * blk, blk)]

        @pl.when(s == 0)
        def _():
            pltpu.make_async_copy(gout.at[npp - 1, c], out, dx_sem.at[c]).start()

        @pl.when(s > 0)
        def _():
            dx_copy(0, c, 0).wait_recv()
            pltpu.make_async_copy(dxin.at[c], out, dx_sem.at[c]).start()

    def out2_copy(i):
        return pltpu.make_async_copy(out2.at[i % 2], g2.at[pl.ds(i * c2, c2), :], o2_sem.at[i % 2])

    def out1_copy(i):
        return pltpu.make_async_copy(out1.at[i % 2], g1.at[:, pl.ds(pl.multiple_of(i * c1, c1), c1)], o1_sem.at[i % 2])

    scale = 1.0 / ndp

    def r2_step(i, _):
        @pl.when(i >= 2)
        def _():
            out2_copy(i - 2).wait()
        rows = pl.ds(pl.multiple_of(p * q2 + i * c2, c2), c2)
        tot = w2v[rows, :].astype(F32)
        for k in order[:-1]:
            send2_copy(i, k).wait()
        for k in range(1, ndp):
            tot = tot + recv2[k - 1, i].astype(F32)
        out2[i % 2] = tot * scale
        out2_copy(i).start()
        return 0

    lax.fori_loop(0, nchunk, r2_step, 0)

    def r1_step(i, _):
        @pl.when(i >= 2)
        def _():
            out1_copy(i - 2).wait()
        rows = pl.ds(pl.multiple_of(p * q1, q1), q1)
        cols = pl.ds(pl.multiple_of(i * c1, c1), c1)
        tot = w1v[rows, cols].astype(F32)
        for k in order[:-1]:
            send1_copy(i, k).wait()
        for k in range(1, ndp):
            tot = tot + recv1[k - 1, i].astype(F32)
        out1[i % 2] = tot * scale
        out1_copy(i).start()
        return 0

    lax.fori_loop(0, nchunk, r1_step, 0)

    for i in range(nchunk - 2, nchunk):
        out2_copy(i).wait()
        out1_copy(i).wait()
    for c in range(nblk):
        pltpu.make_async_copy(dxin.at[c], dx.at[:, pl.ds(c * blk, blk)], dx_sem.at[c]).wait()
    for t in range(npp):
        for c in range(nblk):
            if t < npp - 1:
                @pl.when(npp - 1 - t - s >= 0)
                def _():
                    hop_copy(t, c, 0).wait_send()


def solution(mesh):
    npp = mesh.shape['pp']
    ndp = mesh.shape['dp']

    def body(dy, xs, hs, w1, w2, acc1, acc2):
        tok = dy.shape[1]
        dm, ff = w1.shape[2:]
        ntok = npp * tok
        nchunk = 8
        blk = 256
        nblk = dm // blk
        q1, q2 = dm // ndp, ff // ndp
        c1, c2 = ff // nchunk, q2 // nchunk
        dma = pltpu.SemaphoreType.DMA
        any_spec = pl.BlockSpec(memory_space=pl.ANY)
        r1, r2, dx = pl.pallas_call(
            functools.partial(kernel, npp, ndp, tok, nchunk),
            out_shape=(jax.ShapeDtypeStruct((q1, ff), F32), jax.ShapeDtypeStruct((q2, dm), F32),
                       jax.ShapeDtypeStruct((tok, dm), BF16)),
            in_specs=[any_spec] * 7,
            out_specs=(any_spec,) * 3,
            scratch_shapes=[
                pltpu.VMEM((dm, ff), BF16), pltpu.VMEM((ff, dm), BF16),
                pltpu.VMEM((ndp - 1, nchunk, q1, c1), BF16), pltpu.VMEM((ndp - 1, nchunk, c2, dm), BF16),
                pltpu.VMEM((ntok, ff), BF16), pltpu.VMEM((ntok, dm), BF16),
                pltpu.VMEM((ff, ntok), BF16), pltpu.VMEM((ff, ntok), F32), pltpu.VMEM((ff, ntok), BF16),
                pltpu.VMEM((dm, ntok), BF16), pltpu.VMEM((ntok, dm), BF16),
                pltpu.VMEM((npp, nblk, tok, blk), BF16), pltpu.VMEM((npp, nblk, tok, blk), BF16),
                pltpu.VMEM((nblk, tok, blk), BF16), pltpu.VMEM((blk, blk), BF16),
                pltpu.VMEM((2, ndp, q1, c1), F32), pltpu.VMEM((2, ndp, c2, dm), F32),
                pltpu.VMEM((2, q1, c1), F32), pltpu.VMEM((2, c2, dm), F32),
                dma((1,)), dma((npp,)), dma((8,)), dma((nblk,)), dma((2, ndp)), dma((2, ndp)), dma((2,)), dma((2,)),
                dma((npp, nblk)), dma((npp, nblk)), dma((nblk,)), dma((nblk,)),
                dma((ndp - 1, nchunk)), dma((ndp - 1, nchunk)), dma((ndp - 1, nchunk)), dma((ndp - 1, nchunk)),
            ],
            compiler_params=pltpu.CompilerParams(
                collective_id=0, has_side_effects=True, vmem_limit_bytes=62 * 1024 * 1024),
        )(dy[0], xs.reshape(ntok, dm), hs.reshape(ntok, ff), w1[0, 0], w2[0, 0], acc1[0, 0, 0], acc2[0, 0, 0])
        return r1[None, None], r2[None, None], dx[None]

    spec_row = P(('grp', 'pp'), 'dp', None)
    spec_saved = P(('grp', 'pp'), None, None, 'dp', None)
    spec_w = P(('grp', 'pp'), None, None, None)
    spec_acc = P(('grp', 'pp'), 'dp', None, None, None)
    spec_g = P(('grp', 'pp'), None, 'dp', None)
    return jax.shard_map(body, mesh=mesh, in_specs=(spec_row, spec_saved, spec_saved, spec_w, spec_w, spec_acc, spec_acc), out_specs=(spec_g, spec_g, spec_row), check_vma=False)
```

time: 428 us -> 244 us (0.57); the launches traced: 420 us -> 243 us
  Pallas kernels: 0 us -> 235 us
  waiting for transfers between devices: 178 us -> 0 us
  matrix products: 131 us -> 0 us
  other arithmetic: 35.9 us -> 0 us
  local copies, waits for them, and re-layouts: 34.3 us -> 7.48 us
  starting transfers between devices: 26.5 us -> 0 us
  loops' own time: 12.7 us -> 0 us
    pallas_call x0 -> x1, Pallas kernels: none -> 235 us  [body(): pl.pallas_call(functools.partial(kernel, npp, ndp, tok, nchunk), out_shap...]
    all_to_all x2 -> x0, waiting for transfers between devices: 167 us -> none  [reduce_avg(): recv = lax.all_to_all(pieces, 'dp', 1, 1, tiled=True)]
    dot_general x16 -> x0, matrix products: 131 us -> none  [the longest x4 56 us: layer_back(): dwa = jnp.einsum('td,tf->df', x, dh, preferred_element_type=jnp.float32)]
    convert_element_type x2 -> x0, other arithmetic: 18.1 us -> none  [reduce_avg(): pieces = acc.astype(jnp.bfloat16).reshape(nk, ndp, rows // ndp, cols)]
    unnamed x10 -> x7, local copies, waits for them, and re-layouts: 23 us -> 7.48 us
    all_to_all x2 -> x0, starting transfers between devices: 15.4 us -> none  [reduce_avg(): recv = lax.all_to_all(pieces, 'dp', 1, 1, tiled=True)]
    another operation x8 -> x0, loops' own time: 12.7 us -> none  [the longest x4 11.9 us: body(): lax.cond(j == 0, lambda c: (reduce_avg(c[0], ndp), reduce_avg(c[1], ndp))...]
    reduce_sum x2 -> x0, other arithmetic: 11.3 us -> none  [reduce_avg(): return jnp.sum(recv, axis=1, dtype=jnp.float32) / ndp]
  transfers between devices with their start and end apart: 8 -> 0, of which waited for: 4 -> 0; matrix products, arithmetic and copies ran while one was open for 17% -> 0% of each run, Pallas kernels for 0% -> 0%
where the time goes in v1:
time: 244 us; the launch traced here: 243 us
  Pallas kernels  235 us (96%)
  local copies, waits for them, and re-layouts  7.48 us (3%)
    pallas_call x1, Pallas kernels, body(): pl.pallas_call(functools.partial(kernel, npp, ndp, tok, nchunk), out_shap...  235 us
    unnamed x7, local copies, waits for them, and re-layouts  7.48 us

profile of v1, /device:TPU:1, one launch (start us, length us, event | category | flops | bytes accessed | tf_op | source)
XLA Modules:
  0.0 243.1 jit_solution(14527887880423508802)
XLA Ops:
  0.6 235.0 %shard_map.94 = (f32[256,4096]{1,0:T(8,128)}, f32[1024,1024]{1,0:T(8,128)}, bf16[64,1024]{1,0:T(8,128)(2,1)}) custom-call(bf16[64,1024]{1,0:T(8,128)(2,1)} %bitcast.18, bf16[256,1024]{1,0:T(8,128)(2,1)} %bitcast.17, bf16[256,4096]{1,0:T(8,128)(2,1)} %bitcast.16, bf16[1024,4096]{1,0:T(8,128)(2,1)} %bitcast.12, bf16[4096,1024]{1,0:T(8,128)(2,1)} %bitcast.13, ...), custom_call_target="tpu_custom_call" | custom-call | tf_op jit(solution)/shard_map/pallas_call | solution.py:304
  235.6 0.0 copy-start
  235.7 4.8 %copy.13 = f32[1,1,256,4096]{3,2,1,0:T(8,128)} copy(f32[1,1,256,4096]{3,2,1,0:T(8,128)} %bitcast.15) | data formatting | bytes 8388608
  240.5 0.0 copy-done
  240.5 0.0 copy-start.1
  240.5 2.0 copy.14
  242.5 0.0 copy-done.1
  242.5 0.7 copy.15
Async XLA Ops:
  235.6 4.8 %copy-start = (f32[1024,1024]{1,0:T(8,128)S(1)}, f32[1024,1024]{1,0:T(8,128)}, u32[]{:S(2)}) copy-start(f32[1024,1024]{1,0:T(8,128)} %get-tuple-element.7) | copy-start | bytes 12582916
  240.5 2.0 copy-start.1

commit v2 on v1

v2 whole, which is shorter than its diff:
```python
import functools

import jax
import jax.numpy as jnp
from jax import lax
from jax.experimental import pallas as pl
from jax.experimental.pallas import tpu as pltpu
from jax.sharding import PartitionSpec as P

MESH = pl.DeviceIdType.MESH
NN = (((1,), (0,)), ((), ()))
NT = (((1,), (1,)), ((), ()))
SQRT_2_OVER_PI = 0.7978845608028654
BF16 = jnp.bfloat16
F32 = jnp.float32


def dot(a, b, dims):
    return lax.dot_general(a, b, dims, preferred_element_type=F32)


def kernel(npp, ndp, tok, nchunk, dy, xs, hs, w1, w2, acc1, acc2, g1, g2, dx,
           w1v, w2v, recv1, recv2, hv, xv, act, slope, dht, xt, gt, uacc, first, gin, gout, dxin, ident,
           stage, dyv,
           ld_sem, h_sem, x_sem, w2_sem, w1_sem, st_sem,
           hop_send, hop_recv, dx_recv, send1, recv1_sem, send2, recv2_sem):
    s = lax.axis_index('pp')
    p = lax.axis_index('dp')
    dm, ff = w1v.shape
    blk = ident.shape[0]
    half = 2 * tok
    hb = blk // 2
    nw2 = w2_sem.shape[0]
    w2rows = ff // nw2
    nblk = dm // blk
    q1 = dm // ndp
    q2 = ff // ndp
    rc, cc = first.shape[1:]
    halves = q1 // rc
    mrows = 1024

    far = (p + 2) % ndp
    peer = (p, p + 1 - 2 * (p % 2), far, far + 1 - 2 * (far % 2))

    def w2_copy(i):
        rows = pl.ds(i * w2rows, w2rows)
        return pltpu.make_async_copy(w2.at[rows, :], w2v.at[rows, :], w2_sem.at[i])

    def w1_copy(i):
        rows = pl.ds(i * blk, blk)
        return pltpu.make_async_copy(w1.at[rows, :], w1v.at[rows, :], w1_sem.at[i])

    def rows1(i, k):
        return pl.ds(pl.multiple_of(peer[k] * q1 + (i % halves) * rc, rc), rc)

    def cols1(i):
        return pl.ds(pl.multiple_of((i // halves) * cc, cc), cc)

    def rows2(i, k):
        return pl.ds(pl.multiple_of(peer[k] * q2 + i * rc, rc), rc)

    def acc1_copy(i, k):
        slot = i % 2
        return pltpu.make_async_copy(acc1.at[rows1(i, k), cols1(i)], stage.at[slot, k], st_sem.at[slot, k])

    def acc2_copy(i, k):
        slot = i % 2
        return pltpu.make_async_copy(acc2.at[rows2(i, k), :], stage.at[slot, k], st_sem.at[slot, k])

    def h_copy(t):
        rows = pl.ds((npp - 1 - s - t) * tok, tok)
        return pltpu.make_async_copy(hs.at[rows, :], hv.at[pl.ds(t * tok, tok), :], h_sem.at[t])

    def x_copy(t):
        rows = pl.ds((npp - 1 - s - t) * tok, tok)
        return pltpu.make_async_copy(xs.at[rows, :], xv.at[pl.ds(t * tok, tok), :], x_sem.at[t])

    dy_copy = pltpu.make_async_copy(dy, dyv, ld_sem.at[0])

    def used(t, start):
        @pl.when(t < npp - s)
        def _():
            start(t)

    for t in range(2):
        used(t, lambda t: h_copy(t).start())
    dy_copy.start()

    barrier = pltpu.get_barrier_semaphore()
    for k in range(1, ndp):
        pl.semaphore_signal(barrier, inc=1, device_id={'dp': peer[k]}, device_id_type=MESH)
    for k in range(1, npp):
        pl.semaphore_signal(barrier, inc=1, device_id={'pp': (s + k) % npp}, device_id_type=MESH)

    rid = lax.broadcasted_iota(jnp.int32, (blk, blk), 0)
    cid = lax.broadcasted_iota(jnp.int32, (blk, blk), 1)
    ident[...] = jnp.where(rid == cid, 1.0, 0.0).astype(BF16)
    low = lax.broadcasted_iota(jnp.int32, (hb, half), 1) < tok

    def h_wait(t):
        @pl.when(t < npp - s)
        def _():
            h_copy(t).wait()

        @pl.when(t >= npp - s)
        def _():
            hv[t * tok:(t + 1) * tok, :] = jnp.zeros((tok, ff), BF16)

    def gelu_block(i, lanes):
        rows = pl.ds(pl.multiple_of(i * blk, blk), blk)
        h = dot(ident[...], hv[lanes, rows], NT)
        h2 = h * h
        t = jnp.tanh(SQRT_2_OVER_PI * (h + 0.044715 * (h2 * h)))
        cdf = 0.5 * (1.0 + t)
        act[rows, lanes] = (h * cdf).astype(BF16)
        inner = SQRT_2_OVER_PI * (1.0 + (3.0 * 0.044715) * h2)
        slope[rows, lanes] = cdf + 0.5 * h * ((1.0 + t) * (1.0 - t)) * inner

    def gelu(hh):
        def step(i, _):
            gelu_block(i, slice(hh * half, (hh + 1) * half))
            return 0

        with jax.named_scope('gelu'):
            lax.fori_loop(0, ff // blk, step, 0, unroll=4)

    with jax.named_scope('hwait'):
        for t in range(2):
            h_wait(t)
        dy_copy.wait()
    for i in range(nw2):
        w2_copy(i).start()
    gt[...] = jnp.zeros_like(gt)
    for c in range(nblk):
        gt[c * blk:(c + 1) * blk, 0:tok] = dot(ident[...], dyv[:, c * blk:(c + 1) * blk], NT).astype(BF16)
    for i in range(nblk):
        w1_copy(i).start()
    for t in range(2, npp):
        used(t, lambda t: h_copy(t).start())
    for t in range(npp):
        used(t, lambda t: x_copy(t).start())

    def hop_copy(t, c, to):
        return pltpu.make_async_remote_copy(
            src_ref=gout.at[t, c], dst_ref=gin.at[t, c], send_sem=hop_send.at[t, c], recv_sem=hop_recv.at[t, c],
            device_id={'pp': to}, device_id_type=MESH)

    def dx_copy(t, c, to):
        return pltpu.make_async_remote_copy(
            src_ref=gout.at[t, c], dst_ref=dxin.at[c], send_sem=hop_send.at[t, c], recv_sem=dx_recv.at[c],
            device_id={'pp': to}, device_id_type=MESH)

    def send_first(k):
        return pltpu.make_async_remote_copy(
            src_ref=first.at[k], dst_ref=recv2.at[k - 1, 0], send_sem=send2.at[k - 1, 0], recv_sem=recv2_sem.at[k - 1, 0],
            device_id={'dp': peer[k]}, device_id_type=MESH)

    order = (2, 3, 1, 0)

    def first_chunk():
        with jax.named_scope('first'):
            for k in order:
                acc2_copy(0, k).wait()
                rows = rows2(0, k)
                first[k] = (stage[0, k] + dot(act[rows, :], gt[...], NT)).astype(BF16)
                if k == order[1]:
                    send_first(order[0]).start()
                    send_first(order[1]).start()
            send_first(order[2]).start()
            for k in range(ndp):
                acc2_copy(2, k).start()

    def unpack(packed, c, t):
        lanes = slice((t // 2) * half, (t // 2 + 1) * half)
        v = packed.astype(F32)
        r = pltpu.roll(v, tok, 1)
        for b, (lo, hi) in enumerate(((v, r), (r, v))):
            rows = slice(c * blk + b * hb, c * blk + (b + 1) * hb)
            if t % 2 == 0:
                new = jnp.where(low, lo, 0.0)
            else:
                new = jnp.where(low, gt[rows, lanes].astype(F32), hi)
            gt[rows, lanes] = new.astype(BF16)

    for t in range(npp):
        lanes = slice((t // 2) * half, (t // 2 + 1) * half)

        @pl.when(t < npp - s)
        def _(t=t, lanes=lanes):
            if t == 0:
                def u_step(i, _):
                    w2_copy(i).wait()
                    for b in range(w2rows // blk):
                        gelu_block(i * (w2rows // blk) + b, lanes)
                    rows = pl.ds(pl.multiple_of(i * w2rows, w2rows), w2rows)
                    u = dot(w2v[rows, :], gt[:, lanes], NN)
                    dht[rows, lanes] = (slope[rows, lanes] * u).astype(BF16)
                    return 0

                with jax.named_scope('u0'):
                    lax.fori_loop(0, nw2, u_step, 0)
                with jax.named_scope('barrier'):
                    pl.semaphore_wait(barrier, ndp - 1 + npp - 1)
            else:
                for c in range(nblk):
                    with jax.named_scope('gwait'):
                        hop_copy(t - 1, c, s).wait_recv()
                    unpack(gin[t - 1, c], c, t)
                    if t == npp - 1 and c == nblk - 1:
                        first_chunk()
                    krows = slice(c * blk, (c + 1) * blk)

                    def u_step(i, _):
                        rows = pl.ds(pl.multiple_of(i * mrows, mrows), mrows)
                        u = dot(w2v[rows, krows], gt[krows, lanes], NN)
                        if c > 0:
                            u = uacc[rows, :] + u
                        if c < nblk - 1:
                            uacc[rows, :] = u
                        else:
                            dht[rows, lanes] = (slope[rows, lanes] * u).astype(BF16)
                        return 0

                    with jax.named_scope('u'):
                        lax.fori_loop(0, ff // mrows, u_step, 0, unroll=True)

            def gx_dot(c):
                if t == 0:
                    w1_copy(c).wait()
                rows = slice(c * blk, (c + 1) * blk)
                return gt[rows, lanes].astype(F32) + dot(w1v[rows, :], dht[:, lanes], NN)

            def gx_put(c, z):
                top, bot = z[:hb], z[hb:]
                if t % 2 == 0:
                    z = jnp.where(low, top, pltpu.roll(bot, tok, 1))
                else:
                    z = jnp.where(low, pltpu.roll(top, tok, 1), bot)
                gout[t, c] = z.astype(BF16)

                if t < npp - 1:
                    @pl.when(s > 0)
                    def _():
                        hop_copy(t, c, jnp.maximum(s - 1, 0)).start()

                    @pl.when(s == 0)
                    def _():
                        dx_copy(t, c, npp - 1 - t).start()

            with jax.named_scope('gx'):
                z = gx_dot(0)
                for c in range(1, nblk):
                    z, last = gx_dot(c), z
                    gx_put(c - 1, last)
                gx_put(nblk - 1, z)

        if t == 0:
            for i in range(2):
                for k in range(ndp):
                    acc2_copy(i, k).start()
            @pl.when(s < npp - 2)
            def _():
                for t in range(2, npp):
                    h_wait(t)
                gelu(1)

            @pl.when(s >= npp - 2)
            def _():
                act[:, half:] = jnp.zeros((ff, half), BF16)
                dht[:, half:] = jnp.zeros((ff, half), BF16)

    @pl.when(s > 0)
    def _():
        first_chunk()

    for t in range(npp):
        @pl.when(t < npp - s)
        def _():
            x_copy(t).wait()

        @pl.when(t >= npp - s)
        def _():
            xv[t * tok:(t + 1) * tok, :] = jnp.zeros((tok, dm), BF16)
    for c in range(nblk):
        rows = pl.ds(c * blk, blk)
        xt[rows, :] = dot(ident[...], xv[:, rows], NT).astype(BF16)

    def send2_copy(i, k):
        return pltpu.make_async_remote_copy(
            src_ref=w2v.at[rows2(i, k), :], dst_ref=recv2.at[k - 1, i],
            send_sem=send2.at[k - 1, i], recv_sem=recv2_sem.at[k - 1, i], device_id={'dp': peer[k]}, device_id_type=MESH)

    def send1_copy(i, k):
        return pltpu.make_async_remote_copy(
            src_ref=w1v.at[rows1(i, k), cols1(i)], dst_ref=recv1.at[k - 1, i],
            send_sem=send1.at[k - 1, i], recv_sem=recv1_sem.at[k - 1, i], device_id={'dp': peer[k]}, device_id_type=MESH)

    def a2_step(i, _):
        slot = i % 2
        for k in order:
            acc2_copy(i, k).wait()
            rows = rows2(i, k)
            w2v[rows, :] = (stage[slot, k] + dot(act[rows, :], gt[...], NT)).astype(BF16)
        for k in order[:-1]:
            send2_copy(i, k).start()

        @pl.when(i + 2 < nchunk)
        def _():
            for k in range(ndp):
                acc2_copy(i + 2, k).start()

        @pl.when(i + 2 >= nchunk)
        def _():
            for k in range(ndp):
                acc1_copy(i + 2 - nchunk, k).start()
        return 0

    with jax.named_scope('a2'):
        lax.fori_loop(1, nchunk, a2_step, 0)

    def a1_step(i, _):
        slot = i % 2
        for k in order:
            acc1_copy(i, k).wait()
            w1v[rows1(i, k), cols1(i)] = (
                stage[slot, k] + dot(xt[rows1(i, k), :], dht[cols1(i), :], NT)).astype(BF16)
        for k in order[:-1]:
            send1_copy(i, k).start()

        @pl.when(i + 2 < nchunk)
        def _():
            for k in range(ndp):
                acc1_copy(i + 2, k).start()
        return 0

    with jax.named_scope('a1'):
        lax.fori_loop(0, nchunk, a1_step, 0)

    def put_dx(packed, c, e):
        v = packed.astype(F32)
        r = pltpu.roll(v, tok, 1)
        col = jnp.concatenate([v, r], axis=0).astype(BF16)
        dx[:, c * blk:(c + 1) * blk] = dot(ident[:tok, :half], col, NT).astype(BF16)

    for c in range(nblk):
        @pl.when(s == 0)
        def _():
            put_dx(gout[npp - 1, c], c, 0)

        @pl.when(s > 0)
        def _():
            dx_copy(0, c, 0).wait_recv()
            put_dx(dxin[c], c, 0)

    scale = 1.0 / ndp

    def r2_sum(i, own):
        for k in range(1, ndp):
            own = own + recv2[k - 1, i].astype(F32)
        g2[pl.ds(pl.multiple_of(i * rc, rc), rc), :] = own * scale

    for k in order[:-1]:
        send_first(k).wait()
    r2_sum(0, first[0].astype(F32))

    def r2_step(i, _):
        with jax.named_scope('r2wait'):
            for k in order[:-1]:
                send2_copy(i, k).wait()
        r2_sum(i, w2v[rows2(i, 0), :].astype(F32))
        return 0

    lax.fori_loop(1, nchunk, r2_step, 0)

    def r1_step(i, _):
        with jax.named_scope('r1wait'):
            for k in order[:-1]:
                send1_copy(i, k).wait()
        tot = w1v[rows1(i, 0), cols1(i)].astype(F32)
        for k in range(1, ndp):
            tot = tot + recv1[k - 1, i].astype(F32)
        g1[pl.ds(pl.multiple_of((i % halves) * rc, rc), rc), cols1(i)] = tot * scale
        return 0

    lax.fori_loop(0, nchunk, r1_step, 0)

    for t in range(npp - 1):
        @pl.when(t < npp - s)
        def _():
            for c in range(nblk):
                hop_copy(t, c, 0).wait_send()


def solution(mesh):
    npp = mesh.shape['pp']
    ndp = mesh.shape['dp']

    def body(dy, xs, hs, w1, w2, acc1, acc2):
        tok = dy.shape[1]
        dm, ff = w1.shape[2:]
        ntok = npp * tok
        nchunk = 8
        blk = 256
        nblk = dm // blk
        q1, q2 = dm // ndp, ff // ndp
        rc, cc = q2 // nchunk, dm
        dma = pltpu.SemaphoreType.DMA
        any_spec = pl.BlockSpec(memory_space=pl.ANY)
        vmem = pl.BlockSpec(memory_space=pltpu.VMEM)
        shapes = ((q1, ff), F32), ((q2, dm), F32), ((tok, dm), BF16)
        outs = pl.pallas_call(
            functools.partial(kernel, npp, ndp, tok, nchunk),
            out_shape=tuple(pltpu.VMEM(shape, dtype) for shape, dtype in shapes),
            in_specs=[any_spec] * 7,
            out_specs=(vmem,) * 3,
            scratch_shapes=[
                pltpu.VMEM((dm, ff), BF16), pltpu.VMEM((ff, dm), BF16),
                pltpu.VMEM((ndp - 1, nchunk, rc, cc), BF16), pltpu.VMEM((ndp - 1, nchunk, rc, cc), BF16),
                pltpu.VMEM((ntok, ff), BF16), pltpu.VMEM((ntok, dm), BF16),
                pltpu.VMEM((ff, ntok), BF16), pltpu.VMEM((ff, ntok), F32), pltpu.VMEM((ff, ntok), BF16),
                pltpu.VMEM((dm, ntok), BF16), pltpu.VMEM((dm, ntok), BF16), pltpu.VMEM((ff, 2 * tok), F32),
                pltpu.VMEM((ndp, rc, cc), BF16),
                pltpu.VMEM((npp - 1, nblk, blk // 2, 2 * tok), BF16), pltpu.VMEM((npp, nblk, blk // 2, 2 * tok), BF16),
                pltpu.VMEM((nblk, blk // 2, 2 * tok), BF16), pltpu.VMEM((blk, blk), BF16),
                pltpu.VMEM((2, ndp, rc, cc), F32), pltpu.VMEM((tok, dm), BF16),
                dma((1,)), dma((npp,)), dma((npp,)), dma((8,)), dma((nblk,)), dma((2, ndp)),
                dma((npp - 1, nblk)), dma((npp - 1, nblk)), dma((nblk,)),
                dma((ndp - 1, nchunk)), dma((ndp - 1, nchunk)), dma((ndp - 1, nchunk)), dma((ndp - 1, nchunk)),
            ],
            compiler_params=pltpu.CompilerParams(
                collective_id=0, has_side_effects=True, vmem_limit_bytes=52 * 1024 * 1024),
        )(dy[0], xs.reshape(ntok, dm), hs.reshape(ntok, ff), w1[0, 0], w2[0, 0], acc1[0, 0, 0], acc2[0, 0, 0])
        r1, r2, dx = outs
        return r1[None, None], r2[None, None], dx[None]

    spec_row = P(('grp', 'pp'), 'dp', None)
    spec_saved = P(('grp', 'pp'), None, None, 'dp', None)
    spec_w = P(('grp', 'pp'), None, None, None)
    spec_acc = P(('grp', 'pp'), 'dp', None, None, None)
    spec_g = P(('grp', 'pp'), None, 'dp', None)
    return jax.shard_map(body, mesh=mesh, in_specs=(spec_row, spec_saved, spec_saved, spec_w, spec_w, spec_acc, spec_acc), out_specs=(spec_g, spec_g, spec_row), check_vma=False)
```

time: 244 us -> 218 us (0.89)
  Pallas kernels: 235 us -> 212 us
  local copies, waits for them, and re-layouts: 7.48 us -> 4.68 us
    pallas_call x1, Pallas kernels: 235 us -> 212 us  [body(): pl.pallas_call(functools.partial(kernel, npp, ndp, tok, nchunk), out_shap...]
    unnamed x7 -> x3, local copies, waits for them, and re-layouts: 7.48 us -> 4.68 us
where the time goes in v2:
time: 218 us
  Pallas kernels  212 us (97%)
  local copies, waits for them, and re-layouts  4.68 us (2%)
    pallas_call x1, Pallas kernels, body(): pl.pallas_call(functools.partial(kernel, npp, ndp, tok, nchunk), out_shap...  212 us
    unnamed x3, local copies, waits for them, and re-layouts  4.68 us

profile of v2, /device:TPU:1, one launch (start us, length us, event | category | flops | bytes accessed | tf_op | source)
XLA Modules:
  0.0 217.6 jit_solution(3604101851803911318)
XLA Ops:
  0.6 212.3 %shard_map.94 = (f32[256,4096]{1,0:T(8,128)S(1)}, f32[1024,1024]{1,0:T(8,128)S(1)}, bf16[64,1024]{1,0:T(8,128)(2,1)S(1)}) custom-call(bf16[64,1024]{1,0:T(8,128)(2,1)} %bitcast.19, bf16[256,1024]{1,0:T(8,128)(2,1)} %bitcast.18, bf16[256,4096]{1,0:T(8,128)(2,1)} %bitcast.17, bf16[1024,4096]{1,0:T(8,128)(2,1)} %bitcast.15, bf16[4096,1024]{1,0:T(8,128)(2,1)} %bitcast.16, ...), custom_call_target="tpu_custom_call" | custom-call | tf_op jit(solution)/shard_map/pallas_call | solution.py:411
  212.9 2.0 copy.13
  214.9 2.0 copy.14
  217.0 0.7 copy.15

commit v3 on v2

--- a/solution.py
+++ b/solution.py
@@ -20,10 +20,10 @@
 
 
 def kernel(npp, ndp, tok, nchunk, dy, xs, hs, w1, w2, acc1, acc2, g1, g2, dx,
-           w1v, w2v, recv1, recv2, hv, xv, act, slope, dht, xt, gt, uacc, first, gin, gout, dxin, ident,
+           w1v, w2v, recv1, recv2, hv, xv, act, slope, dht, xt, gt, uacc, first, gin, gout, relay, ident,
            stage, dyv,
            ld_sem, h_sem, x_sem, w2_sem, w1_sem, st_sem,
-           hop_send, hop_recv, dx_recv, send1, recv1_sem, send2, recv2_sem):
+           hop_send, hop_recv, send1, recv1_sem, send2, recv2_sem, unit_send, unit_recv, relay_send, relay_recv):
     s = lax.axis_index('pp')
     p = lax.axis_index('dp')
     dm, ff = w1v.shape
@@ -38,9 +38,14 @@
     rc, cc = first.shape[1:]
     halves = q1 // rc
     mrows = 1024
+    ru = rc // 2
+    shed = (3, 1)
 
     far = (p + 2) % ndp
     peer = (p, p + 1 - 2 * (p % 2), far, far + 1 - 2 * (far % 2))
+
+    far_k = (2, 3)
+    order = far_k + (1, 0)
 
     def w2_copy(i):
         rows = pl.ds(i * w2rows, w2rows)
@@ -85,6 +90,8 @@
     for t in range(2):
         used(t, lambda t: h_copy(t).start())
     dy_copy.start()
+    for i in range(3):
+        w2_copy(i).start()
 
     barrier = pltpu.get_barrier_semaphore()
     for k in range(1, ndp):
@@ -92,6 +99,9 @@
     for k in range(1, npp):
         pl.semaphore_signal(barrier, inc=1, device_id={'pp': (s + k) % npp}, device_id_type=MESH)
 
+    for k in far_k:
+        pl.semaphore_signal(barrier, inc=1, device_id={'pp': npp - 1 - s, 'dp': peer[k]}, device_id_type=MESH)
+
     rid = lax.broadcasted_iota(jnp.int32, (blk, blk), 0)
     cid = lax.broadcasted_iota(jnp.int32, (blk, blk), 1)
     ident[...] = jnp.where(rid == cid, 1.0, 0.0).astype(BF16)
@@ -107,7 +117,7 @@
             hv[t * tok:(t + 1) * tok, :] = jnp.zeros((tok, ff), BF16)
 
     def gelu_block(i, lanes):
-        rows = pl.ds(pl.multiple_of(i * blk, blk), blk)
+        rows = slice(i * blk, (i + 1) * blk) if isinstance(i, int) else pl.ds(pl.multiple_of(i * blk, blk), blk)
         h = dot(ident[...], hv[lanes, rows], NT)
         h2 = h * h
         t = jnp.tanh(SQRT_2_OVER_PI * (h + 0.044715 * (h2 * h)))
@@ -116,46 +126,42 @@
         inner = SQRT_2_OVER_PI * (1.0 + (3.0 * 0.044715) * h2)
         slope[rows, lanes] = cdf + 0.5 * h * ((1.0 + t) * (1.0 - t)) * inner
 
-    def gelu(hh):
+    def gelu(hh, start, stop):
         def step(i, _):
             gelu_block(i, slice(hh * half, (hh + 1) * half))
             return 0
 
         with jax.named_scope('gelu'):
-            lax.fori_loop(0, ff // blk, step, 0, unroll=4)
+            lax.fori_loop(start, stop, step, 0, unroll=4)
 
     with jax.named_scope('hwait'):
         for t in range(2):
             h_wait(t)
         dy_copy.wait()
-    for i in range(nw2):
+    for i in range(3, nw2):
         w2_copy(i).start()
     gt[...] = jnp.zeros_like(gt)
     for c in range(nblk):
         gt[c * blk:(c + 1) * blk, 0:tok] = dot(ident[...], dyv[:, c * blk:(c + 1) * blk], NT).astype(BF16)
-    for i in range(nblk):
-        w1_copy(i).start()
-    for t in range(2, npp):
-        used(t, lambda t: h_copy(t).start())
-    for t in range(npp):
-        used(t, lambda t: x_copy(t).start())
-
-    def hop_copy(t, c, to):
-        return pltpu.make_async_remote_copy(
-            src_ref=gout.at[t, c], dst_ref=gin.at[t, c], send_sem=hop_send.at[t, c], recv_sem=hop_recv.at[t, c],
-            device_id={'pp': to}, device_id_type=MESH)
-
-    def dx_copy(t, c, to):
-        return pltpu.make_async_remote_copy(
-            src_ref=gout.at[t, c], dst_ref=dxin.at[c], send_sem=hop_send.at[t, c], recv_sem=dx_recv.at[c],
-            device_id={'pp': to}, device_id_type=MESH)
+
+    at0 = 1 - jnp.minimum(s, 1)
+
+    def hop_copy(t, c):
+        slot = t + (npp - 1 - t) * at0
+        return pltpu.make_async_remote_copy(
+            src_ref=gout.at[t, c], dst_ref=gin.at[slot, c], send_sem=hop_send.at[t, c], recv_sem=hop_recv.at[slot, c],
+            device_id={'pp': (s - 1) * (1 - at0) + (npp - 1 - t) * at0}, device_id_type=MESH)
+
+    def hop_wait(slot, c):
+        pltpu.make_async_remote_copy(
+            src_ref=gin.at[slot, c], dst_ref=gin.at[slot, c], send_sem=hop_send.at[0, c], recv_sem=hop_recv.at[slot, c],
+            device_id={'pp': s}, device_id_type=MESH).wait_recv()
 
     def send_first(k):
         return pltpu.make_async_remote_copy(
             src_ref=first.at[k], dst_ref=recv2.at[k - 1, 0], send_sem=send2.at[k - 1, 0], recv_sem=recv2_sem.at[k - 1, 0],
             device_id={'dp': peer[k]}, device_id_type=MESH)
 
-    order = (2, 3, 1, 0)
 
     def first_chunk():
         with jax.named_scope('first'):
@@ -188,47 +194,49 @@
         @pl.when(t < npp - s)
         def _(t=t, lanes=lanes):
             if t == 0:
-                def u_step(i, _):
-                    w2_copy(i).wait()
-                    for b in range(w2rows // blk):
-                        gelu_block(i * (w2rows // blk) + b, lanes)
-                    rows = pl.ds(pl.multiple_of(i * w2rows, w2rows), w2rows)
-                    u = dot(w2v[rows, :], gt[:, lanes], NN)
-                    dht[rows, lanes] = (slope[rows, lanes] * u).astype(BF16)
-                    return 0
-
+                gelu(0, 0, ff // blk // 2)
+                for i in range(nblk):
+                    w1_copy(i).start()
+                gelu(0, ff // blk // 2, ff // blk)
                 with jax.named_scope('u0'):
-                    lax.fori_loop(0, nw2, u_step, 0)
+                    for i in range(ff // blk):
+                        if i % (w2rows // blk) == 0:
+                            w2_copy(i // (w2rows // blk)).wait()
+                        rows = slice(i * blk, (i + 1) * blk)
+                        u = dot(w2v[rows, :], gt[:, lanes], NN)
+                        dht[rows, lanes] = (slope[rows, lanes] * u).astype(BF16)
+                for t2 in range(2, npp):
+                    used(t2, lambda t2: h_copy(t2).start())
+                for t2 in range(npp):
+                    used(t2, lambda t2: x_copy(t2).start())
                 with jax.named_scope('barrier'):
-                    pl.semaphore_wait(barrier, ndp - 1 + npp - 1)
+                    pl.semaphore_wait(barrier, ndp - 1 + npp - 1 + len(far_k))
             else:
-                for c in range(nblk):
-                    with jax.named_scope('gwait'):
-                        hop_copy(t - 1, c, s).wait_recv()
-                    unpack(gin[t - 1, c], c, t)
-                    if t == npp - 1 and c == nblk - 1:
+                groups = ((0,), (1,), (2, 3))
+                for group in groups:
+                    for c in group:
+                        with jax.named_scope('gwait'):
+                            hop_wait(t - 1, c)
+                        unpack(gin[t - 1, c], c, t)
+                    if t == npp - 1 and group == groups[-1]:
                         first_chunk()
-                    krows = slice(c * blk, (c + 1) * blk)
-
-                    def u_step(i, _):
-                        rows = pl.ds(pl.multiple_of(i * mrows, mrows), mrows)
-                        u = dot(w2v[rows, krows], gt[krows, lanes], NN)
-                        if c > 0:
-                            u = uacc[rows, :] + u
-                        if c < nblk - 1:
-                            uacc[rows, :] = u
-                        else:
-                            dht[rows, lanes] = (slope[rows, lanes] * u).astype(BF16)
-                        return 0
+                    krows = slice(group[0] * blk, (group[-1] + 1) * blk)
 
                     with jax.named_scope('u'):
-                        lax.fori_loop(0, ff // mrows, u_step, 0, unroll=True)
-
-            def gx_dot(c):
-                if t == 0:
-                    w1_copy(c).wait()
+                        for i in range(ff // mrows):
+                            rows = slice(i * mrows, (i + 1) * mrows)
+                            u = dot(w2v[rows, krows], gt[krows, lanes], NN)
+                            if group != groups[0]:
+                                u = uacc[rows, :] + u
+                            if group != groups[-1]:
+                                uacc[rows, :] = u
+                            else:
+                                dht[rows, lanes] = (slope[rows, lanes] * u).astype(BF16)
+
+            def gx_dot(c, part):
                 rows = slice(c * blk, (c + 1) * blk)
-                return gt[rows, lanes].astype(F32) + dot(w1v[rows, :], dht[:, lanes], NN)
+                k = slice(part * (ff // 2), (part + 1) * (ff // 2))
+                return dot(w1v[rows, k], dht[k, lanes], NN)
 
             def gx_put(c, z):
                 top, bot = z[:hb], z[hb:]
@@ -239,30 +247,30 @@
                 gout[t, c] = z.astype(BF16)
 
                 if t < npp - 1:
-                    @pl.when(s > 0)
-                    def _():
-                        hop_copy(t, c, jnp.maximum(s - 1, 0)).start()
-
-                    @pl.when(s == 0)
-                    def _():
-                        dx_copy(t, c, npp - 1 - t).start()
+                    hop_copy(t, c).start()
 
             with jax.named_scope('gx'):
-                z = gx_dot(0)
-                for c in range(1, nblk):
-                    z, last = gx_dot(c), z
-                    gx_put(c - 1, last)
-                gx_put(nblk - 1, z)
+                last = None
+                for c in range(nblk):
+                    if t == 0 and c % 2 == 0:
+                        w1_copy(c).wait()
+                        w1_copy(c + 1).wait()
+                    if t == 0 and c == 2:
+                        for i in range(2):
+                            for k in range(ndp):
+                                acc2_copy(i, k).start()
+                    z = gt[c * blk:(c + 1) * blk, lanes].astype(F32) + gx_dot(c, 0)
+                    if c > 0:
+                        gx_put(c - 1, last)
+                    last = z + gx_dot(c, 1)
+                gx_put(nblk - 1, last)
 
         if t == 0:
-            for i in range(2):
-                for k in range(ndp):
-                    acc2_copy(i, k).start()
             @pl.when(s < npp - 2)
             def _():
                 for t in range(2, npp):
                     h_wait(t)
-                gelu(1)
+                gelu(1, 0, ff // blk)
 
             @pl.when(s >= npp - 2)
             def _():
@@ -295,28 +303,87 @@
             src_ref=w1v.at[rows1(i, k), cols1(i)], dst_ref=recv1.at[k - 1, i],
             send_sem=send1.at[k - 1, i], recv_sem=recv1_sem.at[k - 1, i], device_id={'dp': peer[k]}, device_id_type=MESH)
 
-    def a2_step(i, _):
-        slot = i % 2
+    units = tuple((u, far_k[u // 2], u % 2) for u in range(4))
+
+    def is_shed(u, stage):
+        cond = jnp.bool_(False)
+        for n, count in enumerate(shed):
+            if u < count:
+                cond = cond | (stage == n)
+        return cond
+
+    def unit_dst(k, b):
+        return recv2.at[k - 1, 1, pl.ds(b * ru, ru), :]
+
+    def unit_src(k, b):
+        return w2v.at[pl.ds(pl.multiple_of(peer[k] * q2 + rc + b * ru, ru), ru), :]
+
+    def unit_copy(u, k, b):
+        return pltpu.make_async_remote_copy(
+            src_ref=unit_src(k, b), dst_ref=unit_dst(k, b), send_sem=unit_send.at[u], recv_sem=unit_recv.at[u],
+            device_id={'dp': peer[k]}, device_id_type=MESH)
+
+    def shed_copy(u, k, b):
+        return pltpu.make_async_remote_copy(
+            src_ref=unit_src(k, b), dst_ref=relay.at[u], send_sem=unit_send.at[u], recv_sem=relay_recv.at[u],
+            device_id={'pp': npp - 1 - s, 'dp': peer[k]}, device_id_type=MESH)
+
+    def relay_copy(u, k, b):
+        return pltpu.make_async_remote_copy(
+            src_ref=relay.at[u], dst_ref=unit_dst(k, b), send_sem=relay_send.at[u], recv_sem=unit_recv.at[u],
+            device_id={'pp': npp - 1 - s}, device_id_type=MESH)
+
+    def send_unit(u, k, b):
+        cond = is_shed(u, s)
+
+        @pl.when(cond)
+        def _():
+            shed_copy(u, k, b).start()
+
+        @pl.when(jnp.logical_not(cond))
+        def _():
+            unit_copy(u, k, b).start()
+
+    def a2_add(i):
         for k in order:
             acc2_copy(i, k).wait()
             rows = rows2(i, k)
-            w2v[rows, :] = (stage[slot, k] + dot(act[rows, :], gt[...], NT)).astype(BF16)
+            w2v[rows, :] = (stage[i % 2, k] + dot(act[rows, :], gt[...], NT)).astype(BF16)
+
+    def a2_next(i):
+        @pl.when(i + 2 < nchunk)
+        def _():
+            for k in range(ndp):
+                acc2_copy(i + 2, k).start()
+
+        @pl.when(i + 2 >= nchunk)
+        def _():
+            for k in range(ndp):
+                acc1_copy(i + 2 - nchunk, k).start()
+
+    def a2_step(i, _):
+        a2_add(i)
         for k in order[:-1]:
             send2_copy(i, k).start()
-
-        @pl.when(i + 2 < nchunk)
-        def _():
-            for k in range(ndp):
-                acc2_copy(i + 2, k).start()
-
-        @pl.when(i + 2 >= nchunk)
-        def _():
-            for k in range(ndp):
-                acc1_copy(i + 2 - nchunk, k).start()
+        a2_next(i)
         return 0
 
     with jax.named_scope('a2'):
-        lax.fori_loop(1, nchunk, a2_step, 0)
+        a2_add(1)
+        for unit in units:
+            send_unit(*unit)
+        send2_copy(1, 1).start()
+        a2_next(jnp.int32(1))
+        lax.fori_loop(2, nchunk, a2_step, 0)
+
+    with jax.named_scope('relay'):
+        for u, k, b in units:
+            @pl.when(is_shed(u, npp - 1 - s))
+            def _():
+                pltpu.make_async_remote_copy(
+                    src_ref=relay.at[u], dst_ref=relay.at[u], send_sem=relay_send.at[u], recv_sem=relay_recv.at[u],
+                    device_id={'pp': npp - 1 - s}, device_id_type=MESH).wait_recv()
+                relay_copy(u, k, b).start()
 
     def a1_step(i, _):
         slot = i % 2
@@ -349,8 +416,8 @@
 
         @pl.when(s > 0)
         def _():
-            dx_copy(0, c, 0).wait_recv()
-            put_dx(dxin[c], c, 0)
+            hop_wait(npp - 1, c)
+            put_dx(gin[npp - 1, c], c, 0)
 
     scale = 1.0 / ndp
 
@@ -362,6 +429,15 @@
     for k in order[:-1]:
         send_first(k).wait()
     r2_sum(0, first[0].astype(F32))
+
+    for u, k, b in units:
+        unit_copy(u, k, b).wait()
+
+        @pl.when(is_shed(u, npp - 1 - s))
+        def _():
+            relay_copy(u, k, b).wait_send()
+    send2_copy(1, 1).wait()
+    r2_sum(1, w2v[rows2(1, 0), :].astype(F32))
 
     def r2_step(i, _):
         with jax.named_scope('r2wait'):
@@ -370,25 +446,42 @@
         r2_sum(i, w2v[rows2(i, 0), :].astype(F32))
         return 0
 
-    lax.fori_loop(1, nchunk, r2_step, 0)
+    lax.fori_loop(2, nchunk, r2_step, 0)
 
     def r1_step(i, _):
         with jax.named_scope('r1wait'):
             for k in order[:-1]:
                 send1_copy(i, k).wait()
-        tot = w1v[rows1(i, 0), cols1(i)].astype(F32)
-        for k in range(1, ndp):
-            tot = tot + recv1[k - 1, i].astype(F32)
-        g1[pl.ds(pl.multiple_of((i % halves) * rc, rc), rc), cols1(i)] = tot * scale
+        with jax.named_scope('r1sum'):
+            tot = w1v[rows1(i, 0), cols1(i)].astype(F32)
+            for k in range(1, ndp):
+                tot = tot + recv1[k - 1, i].astype(F32)
+            g1[pl.ds(pl.multiple_of((i % halves) * rc, rc), rc), cols1(i)] = tot * scale
         return 0
 
     lax.fori_loop(0, nchunk, r1_step, 0)
 
-    for t in range(npp - 1):
-        @pl.when(t < npp - s)
-        def _():
-            for c in range(nblk):
-                hop_copy(t, c, 0).wait_send()
+    with jax.named_scope('tail'):
+        for t in range(npp - 1):
+            @pl.when(t < npp - s)
+            def _():
+                for c in range(nblk):
+                    hop_copy(t, c).wait_send()
+
+
+def put(g1, g2, dx, o1, o2, o3, sems):
+    pieces = 4
+    copies = []
+    for n, (src, dst) in enumerate(((g1, o1), (g2, o2))):
+        size = src.shape[0] // pieces
+        for i in range(pieces):
+            rows = pl.ds(i * size, size)
+            copies.append(pltpu.make_async_copy(src.at[rows, :], dst.at[rows, :], sems.at[n * pieces + i]))
+    copies.append(pltpu.make_async_copy(dx, o3, sems.at[2 * pieces]))
+    for copy in copies:
+        copy.start()
+    for copy in copies:
+        copy.wait()
 
 
 def solution(mesh):
@@ -420,17 +513,25 @@
                 pltpu.VMEM((ff, ntok), BF16), pltpu.VMEM((ff, ntok), F32), pltpu.VMEM((ff, ntok), BF16),
                 pltpu.VMEM((dm, ntok), BF16), pltpu.VMEM((dm, ntok), BF16), pltpu.VMEM((ff, 2 * tok), F32),
                 pltpu.VMEM((ndp, rc, cc), BF16),
-                pltpu.VMEM((npp - 1, nblk, blk // 2, 2 * tok), BF16), pltpu.VMEM((npp, nblk, blk // 2, 2 * tok), BF16),
-                pltpu.VMEM((nblk, blk // 2, 2 * tok), BF16), pltpu.VMEM((blk, blk), BF16),
+                pltpu.VMEM((npp, nblk, blk // 2, 2 * tok), BF16), pltpu.VMEM((npp, nblk, blk // 2, 2 * tok), BF16),
+                pltpu.VMEM((4, rc // 2, cc), BF16), pltpu.VMEM((blk, blk), BF16),
                 pltpu.VMEM((2, ndp, rc, cc), F32), pltpu.VMEM((tok, dm), BF16),
                 dma((1,)), dma((npp,)), dma((npp,)), dma((8,)), dma((nblk,)), dma((2, ndp)),
-                dma((npp - 1, nblk)), dma((npp - 1, nblk)), dma((nblk,)),
+                dma((npp - 1, nblk)), dma((npp, nblk)),
                 dma((ndp - 1, nchunk)), dma((ndp - 1, nchunk)), dma((ndp - 1, nchunk)), dma((ndp - 1, nchunk)),
+                dma((4,)), dma((4,)), dma((4,)), dma((4,)),
             ],
             compiler_params=pltpu.CompilerParams(
                 collective_id=0, has_side_effects=True, vmem_limit_bytes=52 * 1024 * 1024),
         )(dy[0], xs.reshape(ntok, dm), hs.reshape(ntok, ff), w1[0, 0], w2[0, 0], acc1[0, 0, 0], acc2[0, 0, 0])
-        r1, r2, dx = outs
+        r1, r2, dx = pl.pallas_call(
+            put,
+            out_shape=tuple(jax.ShapeDtypeStruct(shape, dtype) for shape, dtype in shapes),
+            in_specs=[any_spec] * 3,
+            out_specs=(any_spec,) * 3,
+            scratch_shapes=[dma((9,))],
+            compiler_params=pltpu.CompilerParams(vmem_limit_bytes=1024 * 1024),
+        )(*outs)
         return r1[None, None], r2[None, None], dx[None]
 
     spec_row = P(('grp', 'pp'), 'dp', None)

time: 218 us -> 210 us (0.963)
  Pallas kernels: 212 us -> 207 us
  local copies, waits for them, and re-layouts: 4.68 us -> 0 us
    pallas_call x1, Pallas kernels: 212 us -> 204 us  [body(): pl.pallas_call(functools.partial(kernel, npp, ndp, tok, nchunk), out_shap...]
    unnamed x3 -> x0, local copies, waits for them, and re-layouts: 4.68 us -> none
    pallas_call x0 -> x1, Pallas kernels: none -> 3.38 us  [body(): pl.pallas_call(put, out_shape=tuple((jax.ShapeDtypeStruct(shape, dtype) f...]
where the time goes in v3:
time: 210 us; the launch traced here: 208 us
  Pallas kernels  207 us (99%)
    pallas_call x1, Pallas kernels, body(): pl.pallas_call(functools.partial(kernel, npp, ndp, tok, nchunk), out_shap...  204 us

profile of v3, /device:TPU:1, one launch (start us, length us, event | category | flops | bytes accessed | tf_op | source)
XLA Modules:
  0.0 208.2 jit_solution(1851697768324123256)
XLA Ops:
  0.6 204.0 %shard_map.94 = (f32[256,4096]{1,0:T(8,128)S(1)}, f32[1024,1024]{1,0:T(8,128)S(1)}, bf16[64,1024]{1,0:T(8,128)(2,1)S(1)}) custom-call(bf16[64,1024]{1,0:T(8,128)(2,1)} %bitcast.16, bf16[256,1024]{1,0:T(8,128)(2,1)} %bitcast.15, bf16[256,4096]{1,0:T(8,128)(2,1)} %bitcast.14, bf16[1024,4096]{1,0:T(8,128)(2,1)} %bitcast.12, bf16[4096,1024]{1,0:T(8,128)(2,1)} %bitcast.13, ...), custom_call_target="tpu_custom_call" | custom-call | tf_op jit(solution)/shard_map/pallas_call | solution.py:504
  204.6 3.4 %shard_map.95 = (f32[256,4096]{1,0:T(8,128)}, f32[1024,1024]{1,0:T(8,128)}, bf16[64,1024]{1,0:T(8,128)(2,1)}) custom-call(f32[256,4096]{1,0:T(8,128)S(1)} %get-tuple-element.9.g1, f32[1024,1024]{1,0:T(8,128)S(1)} %get-tuple-element.10.g2, bf16[64,1024]{1,0:T(8,128)(2,1)S(1)} %get-tuple-element.11.dx), custom_call_target="tpu_custom_call" | custom-call | tf_op jit(solution)/shard_map/pallas_call | solution.py:527

commit v4 on v3

--- a/solution.py
+++ b/solution.py
@@ -8,6 +8,8 @@
 from jax.sharding import PartitionSpec as P
 
 MESH = pl.DeviceIdType.MESH
+EARLY = (3,)
+VMEM_LIMIT = 53 * 1024 * 1024
 NN = (((1,), (0,)), ((), ()))
 NT = (((1,), (1,)), ((), ()))
 SQRT_2_OVER_PI = 0.7978845608028654
@@ -21,9 +23,10 @@
 
 def kernel(npp, ndp, tok, nchunk, dy, xs, hs, w1, w2, acc1, acc2, g1, g2, dx,
            w1v, w2v, recv1, recv2, hv, xv, act, slope, dht, xt, gt, uacc, first, gin, gout, relay, ident,
-           stage, dyv,
-           ld_sem, h_sem, x_sem, w2_sem, w1_sem, st_sem,
-           hop_send, hop_recv, send1, recv1_sem, send2, recv2_sem, unit_send, unit_recv, relay_send, relay_recv):
+           stage1, stage2, early_acc, early_act, early_g, dyv,
+           ld_sem, h_sem, x_sem, w2_sem, w1_sem, st1_sem, st2_sem, hop_send, hop_recv,
+           send1, recv1_sem, send2, recv2_sem, far_recv, unit_recv, relay_send, relay_recv,
+           early_send, early_recv):
     s = lax.axis_index('pp')
     p = lax.axis_index('dp')
     dm, ff = w1v.shape
@@ -35,11 +38,14 @@
     nblk = dm // blk
     q1 = dm // ndp
     q2 = ff // ndp
+    rc1, cc1 = stage1.shape[2:]
     rc, cc = first.shape[1:]
-    halves = q1 // rc
+    halves = q1 // rc1
+    across = dm // cc
     mrows = 1024
-    ru = rc // 2
-    shed = (3, 1)
+    ru = rc // 4
+    shed = (5, 2)
+    early = tuple(zip((nchunk - 1, nchunk - 2), EARLY))
 
     far = (p + 2) % ndp
     peer = (p, p + 1 - 2 * (p % 2), far, far + 1 - 2 * (far % 2))
@@ -56,21 +62,35 @@
         return pltpu.make_async_copy(w1.at[rows, :], w1v.at[rows, :], w1_sem.at[i])
 
     def rows1(i, k):
-        return pl.ds(pl.multiple_of(peer[k] * q1 + (i % halves) * rc, rc), rc)
+        return pl.ds(pl.multiple_of(peer[k] * q1 + (i % halves) * rc1, rc1), rc1)
 
     def cols1(i):
-        return pl.ds(pl.multiple_of((i // halves) * cc, cc), cc)
+        return pl.ds(pl.multiple_of((i // halves) * cc1, cc1), cc1)
 
     def rows2(i, k):
-        return pl.ds(pl.multiple_of(peer[k] * q2 + i * rc, rc), rc)
+        return pl.ds(pl.multiple_of(peer[k] * q2 + (i // across) * rc, rc), rc)
+
+    def cols2(i):
+        return pl.ds(pl.multiple_of((i % across) * cc, cc), cc)
 
     def acc1_copy(i, k):
-        slot = i % 2
-        return pltpu.make_async_copy(acc1.at[rows1(i, k), cols1(i)], stage.at[slot, k], st_sem.at[slot, k])
+        return pltpu.make_async_copy(acc1.at[rows1(i, k), cols1(i)], stage1.at[i % 2, k], st1_sem.at[i % 2])
+
+    def acc1_wait(i):
+        pltpu.make_async_copy(stage1.at[i % 2], stage1.at[i % 2], st1_sem.at[i % 2]).wait()
+
+    def slot2(i, k, n=1):
+        return pl.ds(pl.multiple_of(((i % 2) * ndp + k) * rc, rc), n * rc)
 
     def acc2_copy(i, k):
-        slot = i % 2
-        return pltpu.make_async_copy(acc2.at[rows2(i, k), :], stage.at[slot, k], st_sem.at[slot, k])
+        return pltpu.make_async_copy(acc2.at[rows2(i, k), cols2(i)], slope.at[slot2(i, k), :], st2_sem.at[i % 2])
+
+    def acc2_wait(i):
+        span = slope.at[slot2(i, 0, ndp), :]
+        pltpu.make_async_copy(span, span, st2_sem.at[i % 2]).wait()
+
+    def first_copy(k):
+        return pltpu.make_async_copy(acc2.at[rows2(0, k), cols2(0)], stage2.at[k], st2_sem.at[2])
 
     def h_copy(t):
         rows = pl.ds((npp - 1 - s - t) * tok, tok)
@@ -90,7 +110,7 @@
     for t in range(2):
         used(t, lambda t: h_copy(t).start())
     dy_copy.start()
-    for i in range(3):
+    for i in range(1):
         w2_copy(i).start()
 
     barrier = pltpu.get_barrier_semaphore()
@@ -120,11 +140,11 @@
         rows = slice(i * blk, (i + 1) * blk) if isinstance(i, int) else pl.ds(pl.multiple_of(i * blk, blk), blk)
         h = dot(ident[...], hv[lanes, rows], NT)
         h2 = h * h
-        t = jnp.tanh(SQRT_2_OVER_PI * (h + 0.044715 * (h2 * h)))
-        cdf = 0.5 * (1.0 + t)
-        act[rows, lanes] = (h * cdf).astype(BF16)
-        inner = SQRT_2_OVER_PI * (1.0 + (3.0 * 0.044715) * h2)
-        slope[rows, lanes] = cdf + 0.5 * h * ((1.0 + t) * (1.0 - t)) * inner
+        t = jnp.tanh(h * (SQRT_2_OVER_PI + (SQRT_2_OVER_PI * 0.044715) * h2))
+        cdf = 0.5 + 0.5 * t
+        a = h * cdf
+        act[rows, lanes] = a.astype(BF16)
+        slope[rows, lanes] = cdf + (a * (1.0 - cdf)) * (2.0 * SQRT_2_OVER_PI + (6.0 * SQRT_2_OVER_PI * 0.044715) * h2)
 
     def gelu(hh, start, stop):
         def step(i, _):
@@ -138,9 +158,16 @@
         for t in range(2):
             h_wait(t)
         dy_copy.wait()
-    for i in range(3, nw2):
+    for i in range(1, nw2):
         w2_copy(i).start()
     gt[...] = jnp.zeros_like(gt)
+
+    @pl.when(s >= npp - 2)
+    def _():
+        early_act[:, half:] = jnp.zeros((rc, half), BF16)
+        for n in range(len(early)):
+            early_g[n, :, half:] = jnp.zeros((cc, half), BF16)
+
     for c in range(nblk):
         gt[c * blk:(c + 1) * blk, 0:tok] = dot(ident[...], dyv[:, c * blk:(c + 1) * blk], NT).astype(BF16)
 
@@ -149,32 +176,64 @@
     def hop_copy(t, c):
         slot = t + (npp - 1 - t) * at0
         return pltpu.make_async_remote_copy(
-            src_ref=gout.at[t, c], dst_ref=gin.at[slot, c], send_sem=hop_send.at[t, c], recv_sem=hop_recv.at[slot, c],
+            src_ref=gout.at[t, c], dst_ref=gin.at[slot, c], send_sem=hop_send.at[t], recv_sem=hop_recv.at[slot, c],
             device_id={'pp': (s - 1) * (1 - at0) + (npp - 1 - t) * at0}, device_id_type=MESH)
 
     def hop_wait(slot, c):
         pltpu.make_async_remote_copy(
-            src_ref=gin.at[slot, c], dst_ref=gin.at[slot, c], send_sem=hop_send.at[0, c], recv_sem=hop_recv.at[slot, c],
+            src_ref=gin.at[slot, c], dst_ref=gin.at[slot, c], send_sem=hop_send.at[0], recv_sem=hop_recv.at[slot, c],
             device_id={'pp': s}, device_id_type=MESH).wait_recv()
 
+    slot_of = {1: 0, 3: 1, 2: 2}
+
+    def sems2(i, k):
+        return dict(send_sem=send2.at[1 if k == 2 else 0], recv_sem=far_recv.at[i] if k == 2 else recv2_sem.at[i],
+                    device_id={'dp': peer[k]}, device_id_type=MESH)
+
     def send_first(k):
-        return pltpu.make_async_remote_copy(
-            src_ref=first.at[k], dst_ref=recv2.at[k - 1, 0], send_sem=send2.at[k - 1, 0], recv_sem=recv2_sem.at[k - 1, 0],
-            device_id={'dp': peer[k]}, device_id_type=MESH)
+        return pltpu.make_async_remote_copy(src_ref=first.at[k], dst_ref=recv2.at[slot_of[k], 0], **sems2(0, k))
+
+    hl = (slice(0, half), slice(half, 2 * half))
+
+    def early_on(n):
+        return s < early[n][1]
+
+    def early_copy(what, n, hh, cond_start=True):
+        i = early[n][0]
+        if what == 'acc':
+            src, dst, q = acc2.at[rows2(i, 2), cols2(i)], early_acc.at[n], n
+        elif what == 'act':
+            src, dst, q = act.at[rows2(i, 2), hl[hh]], early_act.at[:, hl[hh]], 2 + hh
+        else:
+            src, dst, q = gt.at[cols2(i), hl[hh]], early_g.at[n, :, hl[hh]], 4 + 2 * n + hh
+        return pltpu.make_async_remote_copy(
+            src_ref=src, dst_ref=dst, send_sem=early_send.at[q], recv_sem=early_recv.at[q],
+            device_id={'dp': peer[2]}, device_id_type=MESH)
+
+    def early_start():
+        for n in range(len(early)):
+            @pl.when(early_on(n))
+            def _():
+                early_copy('acc', n, 0).start()
+                if n == 0:
+                    early_copy('act', 0, 0).start()
+
+    def early_gt(hh, cond=None):
+        for n in range(len(early)):
+            @pl.when(early_on(n) if cond is None else early_on(n) & cond)
+            def _():
+                early_copy('g', n, hh).start()
 
 
     def first_chunk():
         with jax.named_scope('first'):
+            pltpu.make_async_copy(stage2, stage2, st2_sem.at[2]).wait()
             for k in order:
-                acc2_copy(0, k).wait()
-                rows = rows2(0, k)
-                first[k] = (stage[0, k] + dot(act[rows, :], gt[...], NT)).astype(BF16)
+                first[k] = (stage2[k] + dot(act[rows2(0, k), :], gt[0:cc, :], NT)).astype(BF16)
                 if k == order[1]:
                     send_first(order[0]).start()
                     send_first(order[1]).start()
             send_first(order[2]).start()
-            for k in range(ndp):
-                acc2_copy(2, k).start()
 
     def unpack(packed, c, t):
         lanes = slice((t // 2) * half, (t // 2 + 1) * half)
@@ -198,19 +257,28 @@
                 for i in range(nblk):
                     w1_copy(i).start()
                 gelu(0, ff // blk // 2, ff // blk)
+                with jax.named_scope('barrier'):
+                    pl.semaphore_wait(barrier, ndp - 1 + npp - 1 + len(far_k))
+                early_start()
                 with jax.named_scope('u0'):
-                    for i in range(ff // blk):
-                        if i % (w2rows // blk) == 0:
-                            w2_copy(i // (w2rows // blk)).wait()
-                        rows = slice(i * blk, (i + 1) * blk)
-                        u = dot(w2v[rows, :], gt[:, lanes], NN)
-                        dht[rows, lanes] = (slope[rows, lanes] * u).astype(BF16)
+                    for part in range(2):
+                        for b in range(nw2 // 2):
+                            w2_copy(part * (nw2 // 2) + b).wait()
+                        for c in range(nblk):
+                            krows = slice(c * blk, (c + 1) * blk)
+                            for i in range(ff // mrows // 2):
+                                rows = slice(part * (ff // 2) + i * mrows, part * (ff // 2) + (i + 1) * mrows)
+                                u = dot(w2v[rows, krows], gt[krows, lanes], NN)
+                                if c > 0:
+                                    u = uacc[rows, :] + u
+                                if c < nblk - 1:
+                                    uacc[rows, :] = u
+                                else:
+                                    dht[rows, lanes] = (slope[rows, lanes] * u).astype(BF16)
                 for t2 in range(2, npp):
                     used(t2, lambda t2: h_copy(t2).start())
                 for t2 in range(npp):
                     used(t2, lambda t2: x_copy(t2).start())
-                with jax.named_scope('barrier'):
-                    pl.semaphore_wait(barrier, ndp - 1 + npp - 1 + len(far_k))
             else:
                 groups = ((0,), (1,), (2, 3))
                 for group in groups:
@@ -218,8 +286,14 @@
                         with jax.named_scope('gwait'):
                             hop_wait(t - 1, c)
                         unpack(gin[t - 1, c], c, t)
-                    if t == npp - 1 and group == groups[-1]:
-                        first_chunk()
+                    if group == groups[-1]:
+                        if t == npp - 1:
+                            first_chunk()
+                            early_gt(1)
+                        elif t == npp - 2:
+                            early_gt(1, s == 1)
+                        elif t == 1:
+                            early_gt(0)
                     krows = slice(group[0] * blk, (group[-1] + 1) * blk)
 
                     with jax.named_scope('u'):
@@ -256,9 +330,11 @@
                         w1_copy(c).wait()
                         w1_copy(c + 1).wait()
                     if t == 0 and c == 2:
+                        for k in range(ndp):
+                            first_copy(k).start()
                         for i in range(2):
                             for k in range(ndp):
-                                acc2_copy(i, k).start()
+                                acc1_copy(i, k).start()
                     z = gt[c * blk:(c + 1) * blk, lanes].astype(F32) + gx_dot(c, 0)
                     if c > 0:
                         gx_put(c - 1, last)
@@ -272,10 +348,18 @@
                     h_wait(t)
                 gelu(1, 0, ff // blk)
 
+                @pl.when(early_on(0))
+                def _():
+                    early_copy('act', 0, 1).start()
+
             @pl.when(s >= npp - 2)
             def _():
                 act[:, half:] = jnp.zeros((ff, half), BF16)
                 dht[:, half:] = jnp.zeros((ff, half), BF16)
+
+    for i in range(1, 3):
+        for k in range(ndp):
+            acc2_copy(i, k).start()
 
     @pl.when(s > 0)
     def _():
@@ -295,15 +379,14 @@
 
     def send2_copy(i, k):
         return pltpu.make_async_remote_copy(
-            src_ref=w2v.at[rows2(i, k), :], dst_ref=recv2.at[k - 1, i],
-            send_sem=send2.at[k - 1, i], recv_sem=recv2_sem.at[k - 1, i], device_id={'dp': peer[k]}, device_id_type=MESH)
+            src_ref=w2v.at[rows2(i, k), cols2(i)], dst_ref=recv2.at[slot_of[k], i], **sems2(i, k))
 
     def send1_copy(i, k):
         return pltpu.make_async_remote_copy(
-            src_ref=w1v.at[rows1(i, k), cols1(i)], dst_ref=recv1.at[k - 1, i],
-            send_sem=send1.at[k - 1, i], recv_sem=recv1_sem.at[k - 1, i], device_id={'dp': peer[k]}, device_id_type=MESH)
-
-    units = tuple((u, far_k[u // 2], u % 2) for u in range(4))
+            src_ref=w1v.at[rows1(i, k), cols1(i)], dst_ref=recv1.at[i, k - 1],
+            send_sem=send1.at[0], recv_sem=recv1_sem.at[i], device_id={'dp': peer[k]}, device_id_type=MESH)
+
+    units = tuple((u, far_k[u // 4], u % 4) for u in range(8))
 
     def is_shed(u, stage):
         cond = jnp.bool_(False)
@@ -313,19 +396,19 @@
         return cond
 
     def unit_dst(k, b):
-        return recv2.at[k - 1, 1, pl.ds(b * ru, ru), :]
+        return recv2.at[slot_of[k], 1, pl.ds(b * ru, ru), :]
 
     def unit_src(k, b):
-        return w2v.at[pl.ds(pl.multiple_of(peer[k] * q2 + rc + b * ru, ru), ru), :]
+        return w2v.at[pl.ds(pl.multiple_of(peer[k] * q2 + b * ru, ru), ru), cols2(1)]
 
     def unit_copy(u, k, b):
         return pltpu.make_async_remote_copy(
-            src_ref=unit_src(k, b), dst_ref=unit_dst(k, b), send_sem=unit_send.at[u], recv_sem=unit_recv.at[u],
+            src_ref=unit_src(k, b), dst_ref=unit_dst(k, b), send_sem=send2.at[1 if k == 2 else 0], recv_sem=unit_recv.at[u],
             device_id={'dp': peer[k]}, device_id_type=MESH)
 
     def shed_copy(u, k, b):
         return pltpu.make_async_remote_copy(
-            src_ref=unit_src(k, b), dst_ref=relay.at[u], send_sem=unit_send.at[u], recv_sem=relay_recv.at[u],
+            src_ref=unit_src(k, b), dst_ref=relay.at[u], send_sem=send2.at[1 if k == 2 else 0], recv_sem=relay_recv.at[u],
             device_id={'pp': npp - 1 - s, 'dp': peer[k]}, device_id_type=MESH)
 
     def relay_copy(u, k, b):
@@ -345,10 +428,10 @@
             unit_copy(u, k, b).start()
 
     def a2_add(i):
+        acc2_wait(i)
         for k in order:
-            acc2_copy(i, k).wait()
-            rows = rows2(i, k)
-            w2v[rows, :] = (stage[i % 2, k] + dot(act[rows, :], gt[...], NT)).astype(BF16)
+            w2v[rows2(i, k), cols2(i)] = (
+                slope[slot2(i, k), :] + dot(act[rows2(i, k), :], gt[cols2(i), :], NT)).astype(BF16)
 
     def a2_next(i):
         @pl.when(i + 2 < nchunk)
@@ -356,10 +439,7 @@
             for k in range(ndp):
                 acc2_copy(i + 2, k).start()
 
-        @pl.when(i + 2 >= nchunk)
-        def _():
-            for k in range(ndp):
-                acc1_copy(i + 2 - nchunk, k).start()
+    plain = nchunk - len(early)
 
     def a2_step(i, _):
         a2_add(i)
@@ -368,13 +448,28 @@
         a2_next(i)
         return 0
 
+    def far_copy(n):
+        i = early[n][0]
+        return pltpu.make_async_remote_copy(
+            src_ref=w2v.at[rows2(i, 2), cols2(i)], dst_ref=recv2.at[slot_of[2], i],
+            send_sem=send2.at[2 + n], recv_sem=far_recv.at[i], device_id={'dp': peer[2]}, device_id_type=MESH)
+
     with jax.named_scope('a2'):
         a2_add(1)
         for unit in units:
             send_unit(*unit)
         send2_copy(1, 1).start()
         a2_next(jnp.int32(1))
-        lax.fori_loop(2, nchunk, a2_step, 0)
+        lax.fori_loop(2, plain, a2_step, 0)
+        for n in reversed(range(len(early))):
+            i = early[n][0]
+            a2_add(i)
+
+            @pl.when(jnp.logical_not(early_on(n)))
+            def _():
+                far_copy(n).start()
+            for k in (3, 1):
+                send2_copy(i, k).start()
 
     with jax.named_scope('relay'):
         for u, k, b in units:
@@ -386,11 +481,10 @@
                 relay_copy(u, k, b).start()
 
     def a1_step(i, _):
-        slot = i % 2
+        acc1_wait(i)
         for k in order:
-            acc1_copy(i, k).wait()
             w1v[rows1(i, k), cols1(i)] = (
-                stage[slot, k] + dot(xt[rows1(i, k), :], dht[cols1(i), :], NT)).astype(BF16)
+                stage1[i % 2, k] + dot(xt[rows1(i, k), :], dht[cols1(i), :], NT)).astype(BF16)
         for k in order[:-1]:
             send1_copy(i, k).start()
 
@@ -421,52 +515,85 @@
 
     scale = 1.0 / ndp
 
+    def all_of(ref, sem):
+        return pltpu.make_async_copy(ref, ref, sem)
+
     def r2_sum(i, own):
         for k in range(1, ndp):
-            own = own + recv2[k - 1, i].astype(F32)
-        g2[pl.ds(pl.multiple_of(i * rc, rc), rc), :] = own * scale
-
-    for k in order[:-1]:
-        send_first(k).wait()
+            own = own + recv2[slot_of[k], i].astype(F32)
+        rows = pl.ds(pl.multiple_of((i // across) * rc, rc), rc)
+        g2[rows, cols2(i)] = own * scale
+
+    def r2_wait(i):
+        with jax.named_scope('r2wait'):
+            all_of(recv2.at[0:2, i], recv2_sem.at[i]).wait()
+            all_of(recv2.at[2, i], far_recv.at[i]).wait()
+
+    r2_wait(0)
     r2_sum(0, first[0].astype(F32))
 
     for u, k, b in units:
-        unit_copy(u, k, b).wait()
-
-        @pl.when(is_shed(u, npp - 1 - s))
-        def _():
-            relay_copy(u, k, b).wait_send()
-    send2_copy(1, 1).wait()
-    r2_sum(1, w2v[rows2(1, 0), :].astype(F32))
+        all_of(relay.at[u], unit_recv.at[u]).wait()
+    all_of(recv2.at[0, 1], recv2_sem.at[1]).wait()
+    r2_sum(1, w2v[rows2(1, 0), cols2(1)].astype(F32))
 
     def r2_step(i, _):
+        r2_wait(i)
+        r2_sum(i, w2v[rows2(i, 0), cols2(i)].astype(F32))
+        return 0
+
+    lax.fori_loop(2, plain, r2_step, 0)
+
+    for n in reversed(range(len(early))):
+        i = early[n][0]
+
+        @pl.when(early_on(n))
+        def _():
+            early_copy('acc', n, 0).wait()
+            for hh in range(2):
+                if hh == 0:
+                    if n == 0:
+                        early_copy('act', n, hh).wait()
+                    early_copy('g', n, hh).wait()
+                else:
+                    @pl.when(s < npp - 2)
+                    def _():
+                        if n == 0:
+                            early_copy('act', n, hh).wait()
+                        early_copy('g', n, hh).wait()
+            recv2[slot_of[2], i] = (early_acc[n] + dot(early_act[...], early_g[n], NT)).astype(BF16)
+
+        @pl.when(jnp.logical_not(early_on(n)))
+        def _():
+            far_copy(n).wait()
         with jax.named_scope('r2wait'):
-            for k in order[:-1]:
-                send2_copy(i, k).wait()
-        r2_sum(i, w2v[rows2(i, 0), :].astype(F32))
-        return 0
-
-    lax.fori_loop(2, nchunk, r2_step, 0)
+            all_of(recv2.at[0:2, i], recv2_sem.at[i]).wait()
+        r2_sum(i, w2v[rows2(i, 0), cols2(i)].astype(F32))
 
     def r1_step(i, _):
         with jax.named_scope('r1wait'):
-            for k in order[:-1]:
-                send1_copy(i, k).wait()
+            all_of(recv1.at[i], recv1_sem.at[i]).wait()
         with jax.named_scope('r1sum'):
             tot = w1v[rows1(i, 0), cols1(i)].astype(F32)
             for k in range(1, ndp):
-                tot = tot + recv1[k - 1, i].astype(F32)
-            g1[pl.ds(pl.multiple_of((i % halves) * rc, rc), rc), cols1(i)] = tot * scale
+                tot = tot + recv1[i, k - 1].astype(F32)
+            g1[pl.ds(pl.multiple_of((i % halves) * rc1, rc1), rc1), cols1(i)] = tot * scale
         return 0
 
     lax.fori_loop(0, nchunk, r1_step, 0)
 
     with jax.named_scope('tail'):
+        all_of(recv1, send1.at[0]).wait()
+        all_of(recv2.at[0:2], send2.at[0]).wait()
+        all_of(recv2.at[2, 0:plain], send2.at[1]).wait()
+        for u, k, b in units:
+            @pl.when(is_shed(u, npp - 1 - s))
+            def _():
+                relay_copy(u, k, b).wait_send()
         for t in range(npp - 1):
             @pl.when(t < npp - s)
             def _():
-                for c in range(nblk):
-                    hop_copy(t, c).wait_send()
+                all_of(gout.at[t], hop_send.at[t]).wait()
 
 
 def put(g1, g2, dx, o1, o2, o3, sems):
@@ -496,7 +623,8 @@
         blk = 256
         nblk = dm // blk
         q1, q2 = dm // ndp, ff // ndp
-        rc, cc = q2 // nchunk, dm
+        rc1, cc1 = q1 // 2, ff // (nchunk // 2)
+        rc, cc = q2 // 2, dm // (nchunk // 2)
         dma = pltpu.SemaphoreType.DMA
         any_spec = pl.BlockSpec(memory_space=pl.ANY)
         vmem = pl.BlockSpec(memory_space=pltpu.VMEM)
@@ -508,21 +636,23 @@
             out_specs=(vmem,) * 3,
             scratch_shapes=[
                 pltpu.VMEM((dm, ff), BF16), pltpu.VMEM((ff, dm), BF16),
-                pltpu.VMEM((ndp - 1, nchunk, rc, cc), BF16), pltpu.VMEM((ndp - 1, nchunk, rc, cc), BF16),
+                pltpu.VMEM((nchunk, ndp - 1, rc1, cc1), BF16), pltpu.VMEM((ndp - 1, nchunk, rc, cc), BF16),
                 pltpu.VMEM((ntok, ff), BF16), pltpu.VMEM((ntok, dm), BF16),
                 pltpu.VMEM((ff, ntok), BF16), pltpu.VMEM((ff, ntok), F32), pltpu.VMEM((ff, ntok), BF16),
                 pltpu.VMEM((dm, ntok), BF16), pltpu.VMEM((dm, ntok), BF16), pltpu.VMEM((ff, 2 * tok), F32),
                 pltpu.VMEM((ndp, rc, cc), BF16),
                 pltpu.VMEM((npp, nblk, blk // 2, 2 * tok), BF16), pltpu.VMEM((npp, nblk, blk // 2, 2 * tok), BF16),
-                pltpu.VMEM((4, rc // 2, cc), BF16), pltpu.VMEM((blk, blk), BF16),
-                pltpu.VMEM((2, ndp, rc, cc), F32), pltpu.VMEM((tok, dm), BF16),
-                dma((1,)), dma((npp,)), dma((npp,)), dma((8,)), dma((nblk,)), dma((2, ndp)),
-                dma((npp - 1, nblk)), dma((npp, nblk)),
-                dma((ndp - 1, nchunk)), dma((ndp - 1, nchunk)), dma((ndp - 1, nchunk)), dma((ndp - 1, nchunk)),
-                dma((4,)), dma((4,)), dma((4,)), dma((4,)),
+                pltpu.VMEM((8, rc // 4, cc), BF16), pltpu.VMEM((blk, blk), BF16),
+                pltpu.VMEM((2, ndp, rc1, cc1), F32), pltpu.VMEM((ndp, rc, cc), F32),
+                pltpu.VMEM((len(EARLY), rc, cc), F32), pltpu.VMEM((rc, ntok), BF16), pltpu.VMEM((len(EARLY), cc, ntok), BF16),
+                pltpu.VMEM((tok, dm), BF16),
+                dma((1,)), dma((npp,)), dma((npp,)), dma((8,)), dma((nblk,)), dma((2,)), dma((3,)),
+                dma((npp - 1,)), dma((npp, nblk)),
+                dma((1,)), dma((nchunk,)), dma((4,)), dma((nchunk,)), dma((nchunk,)), dma((8,)), dma((8,)), dma((8,)),
+                dma((8,)), dma((8,)),
             ],
             compiler_params=pltpu.CompilerParams(
-                collective_id=0, has_side_effects=True, vmem_limit_bytes=52 * 1024 * 1024),
+                collective_id=0, has_side_effects=True, vmem_limit_bytes=VMEM_LIMIT),
         )(dy[0], xs.reshape(ntok, dm), hs.reshape(ntok, ff), w1[0, 0], w2[0, 0], acc1[0, 0, 0], acc2[0, 0, 0])
         r1, r2, dx = pl.pallas_call(
             put,

time: 210 us -> 205 us (0.976)
  Pallas kernels: 207 us -> 202 us
    pallas_call x1, Pallas kernels: 204 us -> 199 us  [body(): pl.pallas_call(functools.partial(kernel, npp, ndp, tok, nchunk), out_shap...]
where the time goes in v4:
time: 205 us; the launch traced here: 203 us
  Pallas kernels  202 us (99%)
    pallas_call x1, Pallas kernels, body(): pl.pallas_call(functools.partial(kernel, npp, ndp, tok, nchunk), out_shap...  199 us

profile of v4, /device:TPU:1, one launch (start us, length us, event | category | flops | bytes accessed | tf_op | source)
XLA Modules:
  0.0 202.9 jit_solution(7536090028433664759)
XLA Ops:
  0.6 198.7 %shard_map.94 = (f32[256,4096]{1,0:T(8,128)S(1)}, f32[1024,1024]{1,0:T(8,128)S(1)}, bf16[64,1024]{1,0:T(8,128)(2,1)S(1)}) custom-call(bf16[64,1024]{1,0:T(8,128)(2,1)} %bitcast.16, bf16[256,1024]{1,0:T(8,128)(2,1)} %bitcast.15, bf16[256,4096]{1,0:T(8,128)(2,1)} %bitcast.14, bf16[1024,4096]{1,0:T(8,128)(2,1)} %bitcast.12, bf16[4096,1024]{1,0:T(8,128)(2,1)} %bitcast.13, ...), custom_call_target="tpu_custom_call" | custom-call | tf_op jit(solution)/shard_map/pallas_call | solution.py:632
  199.4 3.4 %shard_map.95 = (f32[256,4096]{1,0:T(8,128)}, f32[1024,1024]{1,0:T(8,128)}, bf16[64,1024]{1,0:T(8,128)(2,1)}) custom-call(f32[256,4096]{1,0:T(8,128)S(1)} %get-tuple-element.9.g1, f32[1024,1024]{1,0:T(8,128)S(1)} %get-tuple-element.10.g2, bf16[64,1024]{1,0:T(8,128)(2,1)S(1)} %get-tuple-element.11.dx), custom_call_target="tpu_custom_call" | custom-call | tf_op jit(solution)/shard_map/pallas_call | solution.py:657

commit v5 on v4

--- a/solution.py
+++ b/solution.py
@@ -154,12 +154,6 @@
         with jax.named_scope('gelu'):
             lax.fori_loop(start, stop, step, 0, unroll=4)
 
-    with jax.named_scope('hwait'):
-        for t in range(2):
-            h_wait(t)
-        dy_copy.wait()
-    for i in range(1, nw2):
-        w2_copy(i).start()
     gt[...] = jnp.zeros_like(gt)
 
     @pl.when(s >= npp - 2)
@@ -168,6 +162,12 @@
         for n in range(len(early)):
             early_g[n, :, half:] = jnp.zeros((cc, half), BF16)
 
+    for i in range(1, nw2):
+        w2_copy(i).start()
+    with jax.named_scope('hwait'):
+        for t in range(2):
+            h_wait(t)
+        dy_copy.wait()
     for c in range(nblk):
         gt[c * blk:(c + 1) * blk, 0:tok] = dot(ident[...], dyv[:, c * blk:(c + 1) * blk], NT).astype(BF16)
 
@@ -215,8 +215,6 @@
             @pl.when(early_on(n))
             def _():
                 early_copy('acc', n, 0).start()
-                if n == 0:
-                    early_copy('act', 0, 0).start()
 
     def early_gt(hh, cond=None):
         for n in range(len(early)):
@@ -254,9 +252,6 @@
         def _(t=t, lanes=lanes):
             if t == 0:
                 gelu(0, 0, ff // blk // 2)
-                for i in range(nblk):
-                    w1_copy(i).start()
-                gelu(0, ff // blk // 2, ff // blk)
                 with jax.named_scope('barrier'):
                     pl.semaphore_wait(barrier, ndp - 1 + npp - 1 + len(far_k))
                 early_start()
@@ -264,6 +259,8 @@
                     for part in range(2):
                         for b in range(nw2 // 2):
                             w2_copy(part * (nw2 // 2) + b).wait()
+                        for i in range(nblk if part == 0 else 0):
+                            w1_copy(i).start()
                         for c in range(nblk):
                             krows = slice(c * blk, (c + 1) * blk)
                             for i in range(ff // mrows // 2):
@@ -275,12 +272,18 @@
                                     uacc[rows, :] = u
                                 else:
                                     dht[rows, lanes] = (slope[rows, lanes] * u).astype(BF16)
+                                if part == 0:
+                                    gelu_block(ff // blk // 2 + c * 2 + i, lanes)
+
+                @pl.when(early_on(0))
+                def _():
+                    early_copy('act', 0, 0).start()
                 for t2 in range(2, npp):
                     used(t2, lambda t2: h_copy(t2).start())
                 for t2 in range(npp):
                     used(t2, lambda t2: x_copy(t2).start())
             else:
-                groups = ((0,), (1,), (2, 3))
+                groups = ((0,), (1,), (2,), (3,))
                 for group in groups:
                     for c in group:
                         with jax.named_scope('gwait'):
@@ -329,7 +332,7 @@
                     if t == 0 and c % 2 == 0:
                         w1_copy(c).wait()
                         w1_copy(c + 1).wait()
-                    if t == 0 and c == 2:
+                    if t == 0 and c == 0:
                         for k in range(ndp):
                             first_copy(k).start()
                         for i in range(2):

time: 205 us -> 204 us (level)
  no operation moved by 1% of the time
where the time goes in v5:
time: 204 us; the launch traced here: 202 us
  Pallas kernels  201 us (99%)
    pallas_call x1, Pallas kernels, body(): pl.pallas_call(functools.partial(kernel, npp, ndp, tok, nchunk), out_shap...  198 us

profile of v5, /device:TPU:1, one launch (start us, length us, event | category | flops | bytes accessed | tf_op | source)
XLA Modules:
  0.0 201.8 jit_solution(5597205507396447107)
XLA Ops:
  0.6 197.6 %shard_map.94 = (f32[256,4096]{1,0:T(8,128)S(1)}, f32[1024,1024]{1,0:T(8,128)S(1)}, bf16[64,1024]{1,0:T(8,128)(2,1)S(1)}) custom-call(bf16[64,1024]{1,0:T(8,128)(2,1)} %bitcast.16, bf16[256,1024]{1,0:T(8,128)(2,1)} %bitcast.15, bf16[256,4096]{1,0:T(8,128)(2,1)} %bitcast.14, bf16[1024,4096]{1,0:T(8,128)(2,1)} %bitcast.12, bf16[4096,1024]{1,0:T(8,128)(2,1)} %bitcast.13, ...), custom_call_target="tpu_custom_call" | custom-call | tf_op jit(solution)/shard_map/pallas_call | solution.py:635
  198.2 3.4 %shard_map.95 = (f32[256,4096]{1,0:T(8,128)}, f32[1024,1024]{1,0:T(8,128)}, bf16[64,1024]{1,0:T(8,128)(2,1)}) custom-call(f32[256,4096]{1,0:T(8,128)S(1)} %get-tuple-element.9.g1, f32[1024,1024]{1,0:T(8,128)S(1)} %get-tuple-element.10.g2, bf16[64,1024]{1,0:T(8,128)(2,1)S(1)} %get-tuple-element.11.dx), custom_call_target="tpu_custom_call" | custom-call | tf_op jit(solution)/shard_map/pallas_call | solution.py:660

commit v6 on v5

--- a/solution.py
+++ b/solution.py
@@ -43,8 +43,7 @@
     halves = q1 // rc1
     across = dm // cc
     mrows = 1024
-    ru = rc // 4
-    shed = (5, 2)
+    shed = (6, 2)
     early = tuple(zip((nchunk - 1, nchunk - 2), EARLY))
 
     far = (p + 2) % ndp
@@ -158,6 +157,8 @@
 
     @pl.when(s >= npp - 2)
     def _():
+        act[:, half:] = jnp.zeros((ff, half), BF16)
+        dht[:, half:] = jnp.zeros((ff, half), BF16)
         early_act[:, half:] = jnp.zeros((rc, half), BF16)
         for n in range(len(early)):
             early_g[n, :, half:] = jnp.zeros((cc, half), BF16)
@@ -259,8 +260,13 @@
                     for part in range(2):
                         for b in range(nw2 // 2):
                             w2_copy(part * (nw2 // 2) + b).wait()
-                        for i in range(nblk if part == 0 else 0):
-                            w1_copy(i).start()
+                        if part == 0:
+                            @pl.when(s == npp - 1)
+                            def _():
+                                for k in range(ndp):
+                                    first_copy(k).start()
+                            for i in range(nblk):
+                                w1_copy(i).start()
                         for c in range(nblk):
                             krows = slice(c * blk, (c + 1) * blk)
                             for i in range(ff // mrows // 2):
@@ -333,13 +339,21 @@
                         w1_copy(c).wait()
                         w1_copy(c + 1).wait()
                     if t == 0 and c == 0:
-                        for k in range(ndp):
-                            first_copy(k).start()
+                        @pl.when(s < npp - 1)
+                        def _():
+                            for k in range(ndp):
+                                first_copy(k).start()
                         for i in range(2):
                             for k in range(ndp):
                                 acc1_copy(i, k).start()
+                    if t == 0 and c == 2:
+                        gx_put(1, last)
+
+                        @pl.when(s == npp - 1)
+                        def _():
+                            first_chunk()
                     z = gt[c * blk:(c + 1) * blk, lanes].astype(F32) + gx_dot(c, 0)
-                    if c > 0:
+                    if c > 0 and not (t == 0 and c == 2):
                         gx_put(c - 1, last)
                     last = z + gx_dot(c, 1)
                 gx_put(nblk - 1, last)
@@ -355,16 +369,11 @@
                 def _():
                     early_copy('act', 0, 1).start()
 
-            @pl.when(s >= npp - 2)
-            def _():
-                act[:, half:] = jnp.zeros((ff, half), BF16)
-                dht[:, half:] = jnp.zeros((ff, half), BF16)
-
     for i in range(1, 3):
         for k in range(ndp):
             acc2_copy(i, k).start()
 
-    @pl.when(s > 0)
+    @pl.when((s > 0) & (s < npp - 1))
     def _():
         first_chunk()
 
@@ -389,7 +398,8 @@
             src_ref=w1v.at[rows1(i, k), cols1(i)], dst_ref=recv1.at[i, k - 1],
             send_sem=send1.at[0], recv_sem=recv1_sem.at[i], device_id={'dp': peer[k]}, device_id_type=MESH)
 
-    units = tuple((u, far_k[u // 4], u % 4) for u in range(8))
+    pieces = ((0, rc // 4), (rc // 4, rc // 8), (3 * rc // 8, rc // 8), (rc // 2, rc // 2))
+    units = tuple((u, far_k[u // 4], pieces[u % 4]) for u in range(8))
 
     def is_shed(u, stage):
         cond = jnp.bool_(False)
@@ -399,10 +409,13 @@
         return cond
 
     def unit_dst(k, b):
-        return recv2.at[slot_of[k], 1, pl.ds(b * ru, ru), :]
+        return recv2.at[slot_of[k], 1, pl.ds(*b), :]
 
     def unit_src(k, b):
-        return w2v.at[pl.ds(pl.multiple_of(peer[k] * q2 + b * ru, ru), ru), cols2(1)]
+        return w2v.at[pl.ds(pl.multiple_of(peer[k] * q2 + b[0], rc // 8), b[1]), cols2(1)]
+
+    def relay_at(k, b):
+        return relay.at[far_k.index(k), pl.ds(*b), :]
 
     def unit_copy(u, k, b):
         return pltpu.make_async_remote_copy(
@@ -411,12 +424,12 @@
 
     def shed_copy(u, k, b):
         return pltpu.make_async_remote_copy(
-            src_ref=unit_src(k, b), dst_ref=relay.at[u], send_sem=send2.at[1 if k == 2 else 0], recv_sem=relay_recv.at[u],
+            src_ref=unit_src(k, b), dst_ref=relay_at(k, b), send_sem=send2.at[1 if k == 2 else 0], recv_sem=relay_recv.at[u],
             device_id={'pp': npp - 1 - s, 'dp': peer[k]}, device_id_type=MESH)
 
     def relay_copy(u, k, b):
         return pltpu.make_async_remote_copy(
-            src_ref=relay.at[u], dst_ref=unit_dst(k, b), send_sem=relay_send.at[u], recv_sem=unit_recv.at[u],
+            src_ref=relay_at(k, b), dst_ref=unit_dst(k, b), send_sem=relay_send.at[u], recv_sem=unit_recv.at[u],
             device_id={'pp': npp - 1 - s}, device_id_type=MESH)
 
     def send_unit(u, k, b):
@@ -479,7 +492,7 @@
             @pl.when(is_shed(u, npp - 1 - s))
             def _():
                 pltpu.make_async_remote_copy(
-                    src_ref=relay.at[u], dst_ref=relay.at[u], send_sem=relay_send.at[u], recv_sem=relay_recv.at[u],
+                    src_ref=relay_at(k, b), dst_ref=relay_at(k, b), send_sem=relay_send.at[u], recv_sem=relay_recv.at[u],
                     device_id={'pp': npp - 1 - s}, device_id_type=MESH).wait_recv()
                 relay_copy(u, k, b).start()
 
@@ -536,7 +549,7 @@
     r2_sum(0, first[0].astype(F32))
 
     for u, k, b in units:
-        all_of(relay.at[u], unit_recv.at[u]).wait()
+        all_of(relay_at(k, b), unit_recv.at[u]).wait()
     all_of(recv2.at[0, 1], recv2_sem.at[1]).wait()
     r2_sum(1, w2v[rows2(1, 0), cols2(1)].astype(F32))
 
@@ -645,7 +658,7 @@
                 pltpu.VMEM((dm, ntok), BF16), pltpu.VMEM((dm, ntok), BF16), pltpu.VMEM((ff, 2 * tok), F32),
                 pltpu.VMEM((ndp, rc, cc), BF16),
                 pltpu.VMEM((npp, nblk, blk // 2, 2 * tok), BF16), pltpu.VMEM((npp, nblk, blk // 2, 2 * tok), BF16),
-                pltpu.VMEM((8, rc // 4, cc), BF16), pltpu.VMEM((blk, blk), BF16),
+                pltpu.VMEM((2, rc, cc), BF16), pltpu.VMEM((blk, blk), BF16),
                 pltpu.VMEM((2, ndp, rc1, cc1), F32), pltpu.VMEM((ndp, rc, cc), F32),
                 pltpu.VMEM((len(EARLY), rc, cc), F32), pltpu.VMEM((rc, ntok), BF16), pltpu.VMEM((len(EARLY), cc, ntok), BF16),
                 pltpu.VMEM((tok, dm), BF16),

time: 204 us -> 203 us (level)
  no operation moved by 1% of the time
where the time goes in v6:
time: 203 us; the launch traced here: 202 us
  Pallas kernels  201 us (99%)
    pallas_call x1, Pallas kernels, body(): pl.pallas_call(functools.partial(kernel, npp, ndp, tok, nchunk), out_shap...  198 us

profile of v6, /device:TPU:1, one launch (start us, length us, event | category | flops | bytes accessed | tf_op | source)
XLA Modules:
  0.0 201.9 jit_solution(15135380608042473142)
XLA Ops:
  0.6 197.7 %shard_map.94 = (f32[256,4096]{1,0:T(8,128)S(1)}, f32[1024,1024]{1,0:T(8,128)S(1)}, bf16[64,1024]{1,0:T(8,128)(2,1)S(1)}) custom-call(bf16[64,1024]{1,0:T(8,128)(2,1)} %bitcast.16, bf16[256,1024]{1,0:T(8,128)(2,1)} %bitcast.15, bf16[256,4096]{1,0:T(8,128)(2,1)} %bitcast.14, bf16[1024,4096]{1,0:T(8,128)(2,1)} %bitcast.12, bf16[4096,1024]{1,0:T(8,128)(2,1)} %bitcast.13, ...), custom_call_target="tpu_custom_call" | custom-call | tf_op jit(solution)/shard_map/pallas_call | solution.py:648
  198.3 3.4 %shard_map.95 = (f32[256,4096]{1,0:T(8,128)}, f32[1024,1024]{1,0:T(8,128)}, bf16[64,1024]{1,0:T(8,128)(2,1)}) custom-call(f32[256,4096]{1,0:T(8,128)S(1)} %get-tuple-element.9.g1, f32[1024,1024]{1,0:T(8,128)S(1)} %get-tuple-element.10.g2, bf16[64,1024]{1,0:T(8,128)(2,1)S(1)} %get-tuple-element.11.dx), custom_call_target="tpu_custom_call" | custom-call | tf_op jit(solution)/shard_map/pallas_call | solution.py:673

commit v7 on v6

--- a/solution.py
+++ b/solution.py
@@ -33,7 +33,7 @@
     blk = ident.shape[0]
     half = 2 * tok
     hb = blk // 2
-    nw2 = w2_sem.shape[0]
+    nw2 = 8
     w2rows = ff // nw2
     nblk = dm // blk
     q1 = dm // ndp
@@ -54,7 +54,7 @@
 
     def w2_copy(i):
         rows = pl.ds(i * w2rows, w2rows)
-        return pltpu.make_async_copy(w2.at[rows, :], w2v.at[rows, :], w2_sem.at[i])
+        return pltpu.make_async_copy(w2.at[rows, :], w2v.at[rows, :], w2_sem.at[i * 2 // nw2])
 
     def w1_copy(i):
         rows = pl.ds(i * blk, blk)
@@ -258,8 +258,8 @@
                 early_start()
                 with jax.named_scope('u0'):
                     for part in range(2):
-                        for b in range(nw2 // 2):
-                            w2_copy(part * (nw2 // 2) + b).wait()
+                        w2half = w2v.at[pl.ds(part * (ff // 2), ff // 2), :]
+                        pltpu.make_async_copy(w2half, w2half, w2_sem.at[part]).wait()
                         if part == 0:
                             @pl.when(s == npp - 1)
                             def _():
@@ -352,9 +352,9 @@
                         @pl.when(s == npp - 1)
                         def _():
                             first_chunk()
-                    z = gt[c * blk:(c + 1) * blk, lanes].astype(F32) + gx_dot(c, 0)
                     if c > 0 and not (t == 0 and c == 2):
                         gx_put(c - 1, last)
+                    z = gt[c * blk:(c + 1) * blk, lanes].astype(F32) + gx_dot(c, 0)
                     last = z + gx_dot(c, 1)
                 gx_put(nblk - 1, last)
 
@@ -662,7 +662,7 @@
                 pltpu.VMEM((2, ndp, rc1, cc1), F32), pltpu.VMEM((ndp, rc, cc), F32),
                 pltpu.VMEM((len(EARLY), rc, cc), F32), pltpu.VMEM((rc, ntok), BF16), pltpu.VMEM((len(EARLY), cc, ntok), BF16),
                 pltpu.VMEM((tok, dm), BF16),
-                dma((1,)), dma((npp,)), dma((npp,)), dma((8,)), dma((nblk,)), dma((2,)), dma((3,)),
+                dma((1,)), dma((npp,)), dma((npp,)), dma((2,)), dma((nblk,)), dma((2,)), dma((3,)),
                 dma((npp - 1,)), dma((npp, nblk)),
                 dma((1,)), dma((nchunk,)), dma((4,)), dma((nchunk,)), dma((nchunk,)), dma((8,)), dma((8,)), dma((8,)),
                 dma((8,)), dma((8,)),

time: 203 us -> 203 us (level)
  no operation moved by 1% of the time
where the time goes in v7:
time: 203 us
  Pallas kernels  202 us (100%)
    pallas_call x1, Pallas kernels, body(): pl.pallas_call(functools.partial(kernel, npp, ndp, tok, nchunk), out_shap...  199 us

profile of v7, /device:TPU:1, one launch (start us, length us, event | category | flops | bytes accessed | tf_op | source)
XLA Modules:
  0.0 202.7 jit_solution(15058943013731830024)
XLA Ops:
  0.6 198.5 %shard_map.94 = (f32[256,4096]{1,0:T(8,128)S(1)}, f32[1024,1024]{1,0:T(8,128)S(1)}, bf16[64,1024]{1,0:T(8,128)(2,1)S(1)}) custom-call(bf16[64,1024]{1,0:T(8,128)(2,1)} %bitcast.16, bf16[256,1024]{1,0:T(8,128)(2,1)} %bitcast.15, bf16[256,4096]{1,0:T(8,128)(2,1)} %bitcast.14, bf16[1024,4096]{1,0:T(8,128)(2,1)} %bitcast.12, bf16[4096,1024]{1,0:T(8,128)(2,1)} %bitcast.13, ...), custom_call_target="tpu_custom_call" | custom-call | tf_op jit(solution)/shard_map/pallas_call | solution.py:648
  199.2 3.4 %shard_map.95 = (f32[256,4096]{1,0:T(8,128)}, f32[1024,1024]{1,0:T(8,128)}, bf16[64,1024]{1,0:T(8,128)(2,1)}) custom-call(f32[256,4096]{1,0:T(8,128)S(1)} %get-tuple-element.9.g1, f32[1024,1024]{1,0:T(8,128)S(1)} %get-tuple-element.10.g2, bf16[64,1024]{1,0:T(8,128)(2,1)S(1)} %get-tuple-element.11.dx), custom_call_target="tpu_custom_call" | custom-call | tf_op jit(solution)/shard_map/pallas_call | solution.py:673
